TPU v7x, 32 devices: a whole 2x2x4 slice. The times are simulated.
32 devices in a mesh: gx: 4 (over z), gy: 2 (over core), ta: 4 (over y, x).
Axes of the slice: x: 2, y: 2, z: 4, core: 2. Of those that a mesh axis runs over, the one named last changes fastest.
Arguments:
- links: float32 [4, 2, 3, 3, 8, 4, 4, 128], P(None, None, None, None, 'gx', 'gy', 'ta'), may hold values from -1 to 1, as said below
Outputs:
- flowed: float32 [4, 2, 3, 3, 8, 4, 4, 128], P(None, None, None, None, 'gx', 'gy', 'ta')
- action_slices: float32 [4], P('ta')
Inputs may be any that keep to these rules, and one draw needn't show every extreme that they name: `links`: every link is a special unitary 3x3 matrix.
All inputs are finite; a program needn't handle non-finite values.
Results may differ from a plain program's by a relative error of at most 0.0003.
Values sent between devices are 32-bit elements; how exact they have to be, the bound alone decides.
A program may use at most 64 MiB of HBM per device.

v0:
```python
import functools

import jax
import jax.numpy as jnp
from jax import lax
from jax.experimental import pallas as pl
from jax.experimental.pallas import tpu as pltpu
from jax.sharding import PartitionSpec as P

MESH = pl.DeviceIdType.MESH
AXES = ("gx", "gy", "ta")
flow_eps = 0.1
FRESH = (1.0 / 4.0, 8.0 / 9.0, 3.0 / 4.0)
KEPT = (0.0, -17.0 / 9.0, -1.0)


def mul(a, b):
    def dot(x, y):
        return sum(x[:, k][:, None] * y[k][None] for k in range(3))

    return dot(a[0], b[0]) - dot(a[1], b[1]), dot(a[0], b[1]) + dot(a[1], b[0])


def mul_right_adjoint(a, b):
    def dot(x, y):
        return sum(x[:, k][:, None] * y[:, k][None] for k in range(3))

    return dot(a[0], b[0]) + dot(a[1], b[1]), dot(a[1], b[0]) - dot(a[0], b[1])


def mul_left_adjoint(a, b):
    def dot(x, y):
        return sum(x[k][:, None] * y[k][None] for k in range(3))

    return dot(a[0], b[0]) + dot(a[1], b[1]), dot(a[0], b[1]) - dot(a[1], b[0])


def add(a, b):
    return b if a is None else (a[0] + b[0], a[1] + b[1])


def projected(m):
    r, i = m
    third = (i[0, 0] + i[1, 1] + i[2, 2]) / 3.0
    parts = [i[j, j] - third for j in range(2)]
    for j, k in ((0, 1), (0, 2), (1, 2)):
        parts += [(r[j, k] - r[k, j]) / 2.0, (i[j, k] + i[k, j]) / 2.0]
    return jnp.stack(parts)


def exponential(g):
    h = [g[0], g[1], -(g[0] + g[1])]
    u, v, w = (g[2], g[3]), (g[4], g[5]), (g[6], g[7])
    nu, nv, nw = (z[0] * z[0] + z[1] * z[1] for z in (u, v, w))
    uw = (u[0] * w[0] - u[1] * w[1], u[0] * w[1] + u[1] * w[0])
    diag = [h[0] * h[0] + nu + nv, h[1] * h[1] + nu + nw, h[2] * h[2] + nv + nw]
    p = -0.5 * (diag[0] + diag[1] + diag[2])
    det = (
        h[0] * (h[1] * h[2] - nw)
        - h[1] * nv
        - h[2] * nu
        + 2.0 * (uw[1] * v[0] - uw[0] * v[1])
    )
    s01, s02, s12 = h[0] + h[1], h[0] + h[2], h[1] + h[2]
    square = {
        (0, 1): (
            -s01 * u[1] - (v[0] * w[0] + v[1] * w[1]),
            s01 * u[0] - (v[1] * w[0] - v[0] * w[1]),
        ),
        (0, 2): (-s02 * v[1] + uw[0], s02 * v[0] + uw[1]),
        (1, 2): (
            -s12 * w[1] - (u[0] * v[0] + u[1] * v[1]),
            s12 * w[0] - (u[0] * v[1] - u[1] * v[0]),
        ),
    }
    line = {(0, 1): u, (0, 2): v, (1, 2): w}
    ai4, br4 = det * (-1.0 / 120.0), 0.25 + p * (1.0 / 120.0)
    ai3, br3, bi3, cr3 = (
        det * (-1.0 / 60.0),
        1.0 / 3.0 + p * (1.0 / 60.0),
        ai4 * (1.0 / 3.0),
        br4 * (1.0 / 3.0),
    )
    ai2, br2, bi2, cr2, ci2 = (
        det * cr3 * -0.5,
        0.5 + 0.5 * p * cr3,
        0.5 * ai3,
        0.5 * br3,
        0.5 * bi3,
    )
    ar, ai = 1.0 + det * ci2, -det * cr2
    br, bi, cr, ci = 1.0 + p * cr2, ai2 + p * ci2, br2, bi2
    re = [[None] * 3 for _ in range(3)]
    im = [[None] * 3 for _ in range(3)]
    for j in range(3):
        re[j][j] = ar - bi * h[j] - cr * diag[j]
        im[j][j] = ai + br * h[j] - ci * diag[j]
    for j, k in line:
        x, s = line[j, k], square[j, k]
        even_r, odd_r = br * x[0], bi * x[1]
        even_i, odd_i = br * x[1], bi * x[0]
        cs = (cr * s[0], ci * s[1], cr * s[1], ci * s[0])
        re[j][k] = (even_r - odd_r) + (cs[0] - cs[1])
        im[j][k] = (even_i + odd_i) + (cs[2] + cs[3])
        re[k][j] = -(even_r + odd_r) + (cs[0] + cs[1])
        im[k][j] = (even_i - odd_i) + (cs[3] - cs[2])
    return (
        jnp.stack([jnp.stack(row) for row in re]),
        jnp.stack([jnp.stack(row) for row in im]),
    )


def runs(pairs):
    out = []
    for to, frm in pairs:
        if out and to == out[-1][0] + out[-1][2] and frm == out[-1][1] + out[-1][2]:
            out[-1][2] += 1
        else:
            out.append([to, frm, 1])
    return out


def neighbour_rows(block, offset):
    lx, ly, lt = block
    found = {}
    for row in range(lx * ly * lt):
        site = (row // (ly * lt), row // lt % ly, row % lt)
        moved = [site[k] + offset[k] for k in range(3)]
        step = tuple(moved[k] // block[k] for k in range(3))
        at = [moved[k] % block[k] for k in range(3)]
        frm = (at[0] * ly + at[1]) * lt + at[2]
        found.setdefault(step, []).append((row, frm))
    return found


def unit(k, sign):
    return tuple(sign if j == k else 0 for j in range(3))


PAIRS = [(0, 1), (0, 2), (1, 2)]


def place(m, n):
    return PAIRS.index((min(m, n), max(m, n))), int(m > n)


def plan_of(block):
    remote, local = [], []
    for k in range(3):
        for half, sign in ((0, -1), (1, 1)):
            spans = [(0, 4)]
            if half:
                spans = [(a, b) for a, b in ((0, k), (k + 1, 4)) if b > a]
            for step, pairs in neighbour_rows(block, unit(k, sign)).items():
                for to, frm, n in runs(pairs):
                    for a, b in spans:
                        item = (int(k == 2), "face", k, half, a, b - a, to, frm, n)
                        if any(step):
                            remote.append(item + (step,))
                        else:
                            local.append(item)
    inner = []
    for m in range(3):
        for n in range(3):
            if m == n:
                continue
            c, half = place(m, n)
            ahead, behind = unit(m, 1), unit(n, -1)
            rows_ahead = dict(neighbour_rows(block, ahead).get((0, 0, 0), []))
            rows_behind = dict(neighbour_rows(block, behind).get((0, 0, 0), []))
            offset = tuple(ahead[j] + behind[j] for j in range(3))
            group = 2 * int(2 in (m, n))
            from_minus, from_plus = [], []
            for step, pairs in neighbour_rows(block, offset).items():
                outer = []
                for to, frm in pairs:
                    if to in rows_ahead:
                        from_minus.append((to, rows_ahead[to]))
                    elif to in rows_behind:
                        from_plus.append((to, rows_behind[to]))
                    else:
                        outer.append((to, frm))
                for to, frm, count in runs(outer):
                    remote.append((group, "corner", c, half, n, 1, to, frm, count, step))
            for to, frm, count in runs(sorted(from_minus)):
                inner.append((group, c, half, n, 0, n, to, frm, count))
            for to, frm, count in runs(sorted(from_plus)):
                inner.append((group, c, half, m, 1, n, to, frm, count))
    remote.sort(key=lambda item: (item[1] == "face", -item[0]))
    return remote, local, inner


def kernel(
    block,
    sizes,
    plan,
    partners,
    w_hbm,
    out_ref,
    act_ref,
    w_ref,
    cur_ref,
    face_ref,
    corner_ref,
    gen_ref,
    gen_face_ref,
    gen_corner_ref,
    part_ref,
    slot_ref,
    send_sem,
    recv_sem,
    act_send,
    act_recv,
    load_sem,
):
    remote, local, inner = plan
    rows = block[0] * block[1] * block[2]
    lanes = w_hbm.shape[-1]
    load = pltpu.make_async_copy(w_hbm, w_ref, load_sem)
    load.start()
    here = [lax.axis_index(axis) for axis in AXES]

    def device(step):
        return tuple(lax.rem(here[k] + step[k] + sizes[k], sizes[k]) for k in range(3))

    steps = sorted({item[-1] for item in remote})
    greeted = steps + partners
    barrier = pltpu.get_barrier_semaphore()
    for step in greeted:
        pl.semaphore_signal(barrier, inc=1, device_id=device(step), device_id_type=MESH)
    pl.semaphore_wait(barrier, len(greeted))
    load.wait()

    started, action_copies = [], []

    for stage in range(3):
        field = w_ref if stage == 0 else cur_ref.at[stage - 1]
        copies = []
        for j, item in enumerate(remote):
            group, kind, index, half, first, dirs, to, frm, count, step = item
            span, put, take = pl.ds(first, dirs), pl.ds(half * rows + to, count), pl.ds(frm, count)
            if stage == 0:
                src = w_ref.at[span, :, pl.ds(0, 2), :, take, :]
                if kind == "corner":
                    dst = corner_ref.at[pl.ds(index, 1), :, pl.ds(0, 2), :, put, :]
                else:
                    dst = face_ref.at[index, span, :, pl.ds(0, 2), :, put, :]
            else:
                src = gen_ref.at[stage - 1, span, :, take, :]
                if kind == "corner":
                    dst = gen_corner_ref.at[stage - 1, pl.ds(index, 1), :, put, :]
                else:
                    dst = gen_face_ref.at[stage - 1, index, span, :, put, :]
            copy = pltpu.make_async_remote_copy(
                src_ref=src,
                dst_ref=dst,
                send_sem=send_sem.at[stage, j],
                recv_sem=recv_sem.at[stage, j],
                device_id=device(tuple(-s for s in step)),
                device_id_type=MESH,
            )
            copy.start()
            copies.append((group, copy))
            started.append(copy)
        if stage:
            before = w_ref if stage == 1 else cur_ref.at[stage - 2]
            for mu in range(4):
                own = (before[mu, 0], before[mu, 1])
                moved = mul(exponential(gen_ref[stage - 1, mu]), own)
                cur_ref[stage - 1, mu, 0] = moved[0]
                cur_ref[stage - 1, mu, 1] = moved[1]
        if stage == 1:
            lt = block[2]
            for t in range(lt):
                line = sum(action[r : r + 1] for r in range(t, rows, lt))
                part_ref[t : t + 1, :] = line
            mine = here[0] * sizes[1] + here[1]
            for j, step in enumerate(partners):
                copy = pltpu.make_async_remote_copy(
                    src_ref=part_ref,
                    dst_ref=slot_ref.at[mine],
                    send_sem=act_send.at[j],
                    recv_sem=act_recv.at[j],
                    device_id=device(step),
                    device_id_type=MESH,
                )
                copy.start()
                action_copies.append(copy)
            slot_ref[mine] = part_ref[...]
        for group, kind, index, half, first, dirs, to, frm, count in local:
            low = half * rows + to
            if stage == 0:
                face_ref[index, first : first + dirs, :, 0:2, :, low : low + count, :] = w_ref[
                    first : first + dirs, :, 0:2, :, frm : frm + count, :
                ]
            else:
                gen_face_ref[stage - 1, index, first : first + dirs, :, low : low + count, :] = (
                    gen_ref[stage - 1, first : first + dirs, :, frm : frm + count, :]
                )

        def renew(ref, generator):
            if stage == 0:
                r, i = ref[0, 0:2], ref[1, 0:2]
                for j in range(3):
                    k, l = (j + 1) % 3, (j + 2) % 3
                    ref[0, 2, j] = (r[0, k] * r[1, l] - i[0, k] * i[1, l]) - (
                        r[0, l] * r[1, k] - i[0, l] * i[1, k]
                    )
                    ref[1, 2, j] = (r[0, l] * i[1, k] + i[0, l] * r[1, k]) - (
                        r[0, k] * i[1, l] + i[0, k] * r[1, l]
                    )
            else:
                new = mul(exponential(generator[...]), (ref[0], ref[1]))
                ref[0] = new[0]
                ref[1] = new[1]

        def arrive(wanted):
            for group, copy in copies:
                if group == wanted:
                    copy.wait_recv()
            for k in ((0, 1), (2,), ())[wanted]:
                for mu in range(4):
                    renew(face_ref.at[k, mu], gen_face_ref.at[max(stage - 1, 0), k, mu])
            for c, pair in enumerate(PAIRS):
                if 2 * int(2 in pair) == wanted:
                    renew(corner_ref.at[c], gen_corner_ref.at[max(stage - 1, 0), c])
            for group, c, half, k, side, n, to, frm, count in inner:
                if group == wanted:
                    put, take = half * rows + to, side * rows + frm
                    corner_ref[c, :, :, :, put : put + count, :] = face_ref[
                        k, n, :, :, :, take : take + count, :
                    ]

        def centre(mu):
            return field[mu, 0], field[mu, 1]

        def roll(pair, shift):
            return tuple(pltpu.roll(x, shift % lanes, axis=3) for x in pair)

        def part(ref, index, half):
            low = half * rows
            return tuple(ref[index + (c, slice(None), slice(None), slice(low, low + rows))] for c in range(2))

        def ahead(nu, mu):
            return roll(centre(nu), -1) if mu == 3 else part(face_ref, (mu, nu), 1)

        def behind(mu, nu):
            return part(face_ref, (nu, mu), 0)

        def corner(mu, nu):
            if mu == 3:
                return roll(behind(nu, nu), -1)
            c, half = place(mu, nu)
            return part(corner_ref, (c,), half)

        upper, lower = [None] * 4, [None] * 4
        if stage == 0:
            action = None
        for wanted in (0, 1, 2):
            arrive(wanted)
            for mu in range(4):
                for nu in range(mu + 1, 4):
                    if int(2 in (mu, nu)) != wanted:
                        continue
                    one = mul(centre(mu), ahead(nu, mu))
                    two = mul(centre(nu), ahead(mu, nu))
                    plaq = mul_right_adjoint(one, two)
                    if stage == 0:
                        trace = plaq[0][0, 0] + plaq[0][1, 1] + plaq[0][2, 2]
                        term = 1.0 - trace / 3.0
                        action = term if action is None else action + term
                    flux = projected(plaq)
                    upper[mu] = flux if upper[mu] is None else upper[mu] + flux
                    upper[nu] = -flux if upper[nu] is None else upper[nu] - flux
                    if nu == 3:
                        low = roll(mul_left_adjoint(one, centre(3)), 1)
                        lower[mu] = add(lower[mu], low)
            for mu in range(4):
                for nu in range(3):
                    late = int(2 in (mu, nu)) * (1 if mu == 3 else 2)
                    if nu != mu and late == wanted:
                        one = mul(behind(mu, nu), corner(mu, nu))
                        lower[mu] = add(lower[mu], mul_left_adjoint(one, behind(nu, nu)))
            for mu in ((), (3,), (0, 1, 2))[wanted]:
                omega = projected(mul(centre(mu), lower[mu])) + upper[mu]
                gen = (-flow_eps * FRESH[stage]) * omega
                if stage:
                    gen = gen + KEPT[stage] * gen_ref[stage - 1, mu]
                if stage < 2:
                    gen_ref[stage, mu] = gen
                else:
                    moved = mul(exponential(gen), centre(mu))
                    out_ref[mu, 0] = moved[0]
                    out_ref[mu, 1] = moved[1]
    for copy in started:
        copy.wait_send()
    for copy in action_copies:
        copy.wait()
    total = sum(slot_ref[j] for j in range(sizes[0] * sizes[1]))
    scale = 1.0 / (6.0 * sizes[0] * sizes[1] * block[0] * block[1] * lanes)
    total = jnp.sum(total, axis=1, keepdims=True) * scale
    act_ref[...] = jnp.broadcast_to(total, act_ref.shape)


def solution(mesh):
    sizes = tuple(mesh.shape[axis] for axis in AXES)

    def local(links):
        block = links.shape[4:7]
        lanes = links.shape[7]
        rows = block[0] * block[1] * block[2]
        plan = plan_of(block)
        partners = [
            (i, j, 0) for i in range(sizes[0]) for j in range(sizes[1]) if i or j
        ]
        count = len(plan[0])
        matrix = (2, 3, 3, rows, lanes)
        both = (2, 3, 3, 2 * rows, lanes)
        f32 = jnp.float32
        vmem = pl.BlockSpec(memory_space=pltpu.VMEM)
        flowed, action = pl.pallas_call(
            functools.partial(kernel, block, sizes, plan, partners),
            out_shape=(
                jax.ShapeDtypeStruct((4,) + matrix, f32),
                jax.ShapeDtypeStruct((block[2], lanes), f32),
            ),
            in_specs=[pl.BlockSpec(memory_space=pltpu.HBM)],
            out_specs=(vmem, vmem),
            scratch_shapes=[
                pltpu.VMEM((4,) + matrix, f32),
                pltpu.VMEM((2, 4) + matrix, f32),
                pltpu.VMEM((3, 4) + both, f32),
                pltpu.VMEM((len(PAIRS),) + both, f32),
                pltpu.VMEM((2, 4, 8, rows, lanes), f32),
                pltpu.VMEM((2, 3, 4, 8, 2 * rows, lanes), f32),
                pltpu.VMEM((2, len(PAIRS), 8, 2 * rows, lanes), f32),
                pltpu.VMEM((block[2], lanes), f32),
                pltpu.VMEM((sizes[0] * sizes[1], block[2], lanes), f32),
                pltpu.SemaphoreType.DMA((3, count)),
                pltpu.SemaphoreType.DMA((3, count)),
                pltpu.SemaphoreType.DMA((len(partners),)),
                pltpu.SemaphoreType.DMA((len(partners),)),
                pltpu.SemaphoreType.DMA,
            ],
            compiler_params=pltpu.CompilerParams(
                collective_id=0, has_side_effects=True, vmem_limit_bytes=48 * 2**20
            ),
        )(links.reshape((4,) + matrix))
        return flowed.reshape(links.shape), action[:, 0]

    spec = P(None, None, None, None, "gx", "gy", "ta", None)
    return jax.shard_map(
        local, mesh=mesh, in_specs=(spec,), out_specs=(spec, P("ta")), check_vma=False
    )
```

profile of v0, /device:TPU:0, one launch (start us, length us, event | category | flops | bytes accessed | tf_op | source)
XLA Modules:
  0.0 31.5 jit_solution(14204240929217580476)
XLA Ops:
  0.6 0.0 copy-start
  0.6 0.9 %copy-done = f32[4,2,3,3,2,2,1,128]{7,6,5,4,3,2,1,0:T(1,128)S(1)} copy-done((f32[4,2,3,3,2,2,1,128]{7,6,5,4,3,2,1,0:T(1,128)S(1)}, f32[4,2,3,3,2,2,1,128]{7,6,5,4,3,2,1,0:T(1,128)}, u32[]{:S(2)}) %copy-start) | copy-done | bytes 147480
  1.5 28.1 %shard_map.30 = (f32[4,2,3,3,4,128]{5,4,3,2,1,0:T(4,128)S(1)}, f32[1,128]{1,0:T(1,128)S(1)}) custom-call(f32[4,2,3,3,4,128]{5,4,3,2,1,0:T(4,128)S(1)} %bitcast.6), custom_call_target="tpu_custom_call" | custom-call | tf_op jit(solution)/shard_map/pallas_call | solution.py:421
  29.6 0.7 %copy.6 = f32[4,2,3,3,2,2,1,128]{7,6,5,4,3,2,1,0:T(1,128)} copy(f32[4,2,3,3,2,2,1,128]{7,6,5,4,3,2,1,0:T(1,128)S(1)} %bitcast.7) | data formatting | bytes 294912
Async XLA Ops:
  0.6 0.9 %copy-start = (f32[4,2,3,3,2,2,1,128]{7,6,5,4,3,2,1,0:T(1,128)S(1)}, f32[4,2,3,3,2,2,1,128]{7,6,5,4,3,2,1,0:T(1,128)}, u32[]{:S(2)}) copy-start(f32[4,2,3,3,2,2,1,128]{7,6,5,4,3,2,1,0:T(1,128)} %param.1) | copy-start | bytes 442372
where the time goes:
time: 31.6 us; the launch traced here: 31.5 us
  Pallas kernels  28.1 us (89%)
  between operations  1.81 us (6%)
  local copies, waits for them, and re-layouts  1.57 us (5%)
    pallas_call x1, Pallas kernels, local(): pl.pallas_call(functools.partial(kernel, block, sizes, plan, partners), o...  28.1 us
    unnamed x3, local copies, waits for them, and re-layouts  1.57 us

commit v1 on v0

v1 whole, which is shorter than its diff:
```python
import functools

import jax
import jax.numpy as jnp
from jax import lax
from jax.experimental import pallas as pl
from jax.experimental.pallas import tpu as pltpu
from jax.sharding import PartitionSpec as P

MESH = pl.DeviceIdType.MESH
AXES = ("gx", "gy", "ta")
flow_eps = 0.1
FRESH = (1.0 / 4.0, 8.0 / 9.0, 3.0 / 4.0)
KEPT = (0.0, -17.0 / 9.0, -1.0)


def mul(a, b):
    def dot(x, y):
        return sum(x[:, k][:, None] * y[k][None] for k in range(3))

    return dot(a[0], b[0]) - dot(a[1], b[1]), dot(a[0], b[1]) + dot(a[1], b[0])


def mul_right_adjoint(a, b):
    def dot(x, y):
        return sum(x[:, k][:, None] * y[:, k][None] for k in range(3))

    return dot(a[0], b[0]) + dot(a[1], b[1]), dot(a[1], b[0]) - dot(a[0], b[1])


def mul_left_adjoint(a, b):
    def dot(x, y):
        return sum(x[k][:, None] * y[k][None] for k in range(3))

    return dot(a[0], b[0]) + dot(a[1], b[1]), dot(a[0], b[1]) - dot(a[1], b[0])


def add(a, b):
    return b if a is None else (a[0] + b[0], a[1] + b[1])


def projected(m):
    r, i = m
    third = (i[0, 0] + i[1, 1] + i[2, 2]) / 3.0
    parts = [i[j, j] - third for j in range(2)]
    for j, k in ((0, 1), (0, 2), (1, 2)):
        parts += [(r[j, k] - r[k, j]) / 2.0, (i[j, k] + i[k, j]) / 2.0]
    return jnp.stack(parts)


def exponential(g):
    h = [g[0], g[1], -(g[0] + g[1])]
    u, v, w = (g[2], g[3]), (g[4], g[5]), (g[6], g[7])
    nu, nv, nw = (z[0] * z[0] + z[1] * z[1] for z in (u, v, w))
    uw = (u[0] * w[0] - u[1] * w[1], u[0] * w[1] + u[1] * w[0])
    diag = [h[0] * h[0] + nu + nv, h[1] * h[1] + nu + nw, h[2] * h[2] + nv + nw]
    p = -0.5 * (diag[0] + diag[1] + diag[2])
    det = (
        h[0] * (h[1] * h[2] - nw)
        - h[1] * nv
        - h[2] * nu
        + 2.0 * (uw[1] * v[0] - uw[0] * v[1])
    )
    s01, s02, s12 = h[0] + h[1], h[0] + h[2], h[1] + h[2]
    square = {
        (0, 1): (
            -s01 * u[1] - (v[0] * w[0] + v[1] * w[1]),
            s01 * u[0] - (v[1] * w[0] - v[0] * w[1]),
        ),
        (0, 2): (-s02 * v[1] + uw[0], s02 * v[0] + uw[1]),
        (1, 2): (
            -s12 * w[1] - (u[0] * v[0] + u[1] * v[1]),
            s12 * w[0] - (u[0] * v[1] - u[1] * v[0]),
        ),
    }
    line = {(0, 1): u, (0, 2): v, (1, 2): w}
    ai4, br4 = det * (-1.0 / 120.0), 0.25 + p * (1.0 / 120.0)
    ai3, br3, bi3, cr3 = (
        det * (-1.0 / 60.0),
        1.0 / 3.0 + p * (1.0 / 60.0),
        ai4 * (1.0 / 3.0),
        br4 * (1.0 / 3.0),
    )
    ai2, br2, bi2, cr2, ci2 = (
        det * cr3 * -0.5,
        0.5 + 0.5 * p * cr3,
        0.5 * ai3,
        0.5 * br3,
        0.5 * bi3,
    )
    ar, ai = 1.0 + det * ci2, -det * cr2
    br, bi, cr, ci = 1.0 + p * cr2, ai2 + p * ci2, br2, bi2
    re = [[None] * 3 for _ in range(3)]
    im = [[None] * 3 for _ in range(3)]
    for j in range(3):
        re[j][j] = ar - bi * h[j] - cr * diag[j]
        im[j][j] = ai + br * h[j] - ci * diag[j]
    for j, k in line:
        x, s = line[j, k], square[j, k]
        even_r, odd_r = br * x[0], bi * x[1]
        even_i, odd_i = br * x[1], bi * x[0]
        cs = (cr * s[0], ci * s[1], cr * s[1], ci * s[0])
        re[j][k] = (even_r - odd_r) + (cs[0] - cs[1])
        im[j][k] = (even_i + odd_i) + (cs[2] + cs[3])
        re[k][j] = -(even_r + odd_r) + (cs[0] + cs[1])
        im[k][j] = (even_i - odd_i) + (cs[3] - cs[2])
    return (
        jnp.stack([jnp.stack(row) for row in re]),
        jnp.stack([jnp.stack(row) for row in im]),
    )


def runs(pairs):
    out = []
    for to, frm in pairs:
        if out and to == out[-1][0] + out[-1][2] and frm == out[-1][1] + out[-1][2]:
            out[-1][2] += 1
        else:
            out.append([to, frm, 1])
    return out


def neighbour_rows(block, offset):
    lx, ly, lt = block
    found = {}
    for row in range(lx * ly * lt):
        site = (row // (ly * lt), row // lt % ly, row % lt)
        moved = [site[k] + offset[k] for k in range(3)]
        step = tuple(moved[k] // block[k] for k in range(3))
        at = [moved[k] % block[k] for k in range(3)]
        frm = (at[0] * ly + at[1]) * lt + at[2]
        found.setdefault(step, []).append((row, frm))
    return found


def unit(k, sign):
    return tuple(sign if j == k else 0 for j in range(3))


X, Y, T, Z = 0, 1, 2, 3
PLACE = {X: (0, 0), T: (0, 1), Y: (1, 0), Z: (1, 1)}
BEHIND = {T: 0, X: 3, Y: 7}
BOTH, T_AHEAD, X_AHEAD, Y_AHEAD = 5, 2, 6, 9
CORNER = {(X, T): (11, 0), (T, X): (11, 1), (X, Y): (12, 0), (T, Y): (12, 1), (Y, X): (13, 0), (Y, T): (13, 1)}
SLOTS = 14


def face_at(k, half, d):
    pair, pos = PLACE[d]
    if not half:
        return BEHIND[k] + pair, pos
    if k == Y:
        return Y_AHEAD + pair, pos
    if pair:
        return (X_AHEAD if k == X else T_AHEAD), pos
    return BOTH, int(k == X)


def cover(pairs):
    to, frm = min(pairs)
    assert all(a - b == to - frm for a, b in pairs)
    return to, frm, max(pairs)[0] - to + 1


def plan_of(block):
    rows = block[0] * block[1] * block[2]
    remote, fills = [], []

    def send(group, pair, pairs, frm, count, slot, to, step):
        remote.append((group, pair, pairs, frm, count, slot, to, step))

    for k in range(3):
        for half, sign in ((0, -1), (1, 1)):
            group = "xyt"[k]
            for step, pairs in neighbour_rows(block, unit(k, sign)).items():
                if any(step):
                    to, frm, n = cover(pairs)
                    if k == Y:
                        send(group, 0, 2, frm, rows + n, Y_AHEAD if half else BEHIND[Y], to, step)
                    elif k == X and half:
                        send(group, 0, 2, rows + frm, n, BOTH, rows + to, step)
                        send(group, 1, 1, frm, n, X_AHEAD, to, step)
                    elif k == X:
                        send(group, 0, 2, frm, n, BEHIND[X], to, step)
                        send(group, 0, 2, rows + frm, n, BEHIND[X], rows + to, step)
                    elif half:
                        send(group, 0, 1, frm, n, BOTH, to, step)
                        send(group, 1, 1, frm, rows + n, T_AHEAD, to, step)
                    else:
                        send(group, 0, 2, frm, rows + n, BEHIND[T], to, step)
                    continue
                for d in range(4):
                    if half and d == k:
                        continue
                    slot, pos = face_at(k, half, d)
                    pair, at = PLACE[d]
                    for to, frm, n in runs(pairs):
                        fills.append((group, None, pair, at * rows + frm, slot, pos * rows + to, n))
    for (m, n), (slot, pos) in CORNER.items():
        ahead, behind = unit(m, 1), unit(n, -1)
        rows_ahead = dict(neighbour_rows(block, ahead).get((0, 0, 0), []))
        rows_behind = dict(neighbour_rows(block, behind).get((0, 0, 0), []))
        offset = tuple(ahead[j] + behind[j] for j in range(3))
        group = "c" if Y in (m, n) else "xt"
        pair, at = PLACE[n]
        from_minus, from_plus = [], []
        for step, pairs in neighbour_rows(block, offset).items():
            outer = []
            for to, frm in pairs:
                if to in rows_ahead:
                    from_minus.append((to, rows_ahead[to]))
                elif to in rows_behind:
                    from_plus.append((to, rows_behind[to]))
                else:
                    outer.append((to, frm))
            if outer:
                to, frm, count = cover(outer)
                send(group, pair, 1, at * rows + frm, count, slot, pos * rows + to, step)
        for k, half, found in ((n, 0, from_minus), (m, 1, from_plus)):
            source, side = face_at(k, half, n)
            for to, frm, count in runs(sorted(found)):
                fills.append((group, source, 0, side * rows + frm, slot, pos * rows + to, count))
    remote.sort(key=lambda item: ("xt", "c", "t", "x", "y").index(item[0]))
    return remote, fills


def kernel(
    block,
    sizes,
    plan,
    partners,
    w_hbm,
    out_ref,
    act_ref,
    first_ref,
    cur_ref,
    halo_ref,
    gen_ref,
    gen_halo_ref,
    stack_ref,
    flux_ref,
    part_ref,
    slot_ref,
    send_sem,
    recv_sem,
    act_send,
    act_recv,
    load_sem,
):
    remote, fills = plan
    rows = block[0] * block[1] * block[2]
    lanes = w_hbm.shape[-1]
    loads = []
    for d, (pair, pos) in PLACE.items():
        load = pltpu.make_async_copy(
            w_hbm.at[d], first_ref.at[pair, :, :, :, pl.ds(pos * rows, rows), :], load_sem.at[d]
        )
        load.start()
        loads.append(load)
    here = [lax.axis_index(axis) for axis in AXES]

    def device(step):
        return tuple(lax.rem(here[k] + step[k] + sizes[k], sizes[k]) for k in range(3))

    steps = sorted({item[-1] for item in remote})
    greeted = steps + partners
    barrier = pltpu.get_barrier_semaphore()
    for step in greeted:
        pl.semaphore_signal(barrier, inc=1, device_id=device(step), device_id_type=MESH)
    pl.semaphore_wait(barrier, len(greeted))
    for load in loads:
        load.wait()

    started, action_copies, stacks = [], [], {}

    def low(pos):
        return slice(pos * rows, (pos + 1) * rows)

    def whole(ref, index):
        return ref[index, 0], ref[index, 1]

    def half(ref, index, pos):
        return ref[index, 0, :, :, low(pos), :], ref[index, 1, :, :, low(pos), :]

    def stack(name):
        return stacks.setdefault(name, len(stacks))

    def keep(name, value):
        index = stack(name)
        stack_ref[index, 0], stack_ref[index, 1] = value

    def keep_half(name, pos, value):
        index = stack(name)
        stack_ref[index, 0, :, :, low(pos), :] = value[0]
        stack_ref[index, 1, :, :, low(pos), :] = value[1]

    def twice(name, value):
        keep_half(name, 0, value)
        keep_half(name, 1, value)

    def kept(name):
        return whole(stack_ref, stacks[name])

    def kept_half(name, pos):
        return half(stack_ref, stacks[name], pos)

    def roll(pair, shift):
        return tuple(pltpu.roll(x, shift % lanes, axis=3) for x in pair)

    def face(k, side, d):
        slot, pos = face_at(k, side, d)
        return half(halo_ref, slot, pos)

    for stage in range(3):
        base = first_ref if stage == 0 else cur_ref
        copies = {}
        for j, (group, pair, pairs, frm, count, slot, to, step) in enumerate(remote):
            span, into = pl.ds(pair, pairs), pl.ds(slot, pairs)
            if stage == 0:
                src = first_ref.at[span, :, pl.ds(0, 2), :, pl.ds(frm, count), :]
                dst = halo_ref.at[into, :, pl.ds(0, 2), :, pl.ds(to, count), :]
            else:
                src = gen_ref.at[stage - 1, span, :, pl.ds(frm, count), :]
                dst = gen_halo_ref.at[stage - 1, into, :, pl.ds(to, count), :]
            copy = pltpu.make_async_remote_copy(
                src_ref=src,
                dst_ref=dst,
                send_sem=send_sem.at[stage, j],
                recv_sem=recv_sem.at[stage, j],
                device_id=device(tuple(-s for s in step)),
                device_id_type=MESH,
            )
            copy.start()
            copies.setdefault(group, []).append(copy)
            started.append(copy)

        if stage == 1:
            lt = block[2]
            for t in range(lt):
                part_ref[t : t + 1, :] = sum(action[r : r + 1] for r in range(t, rows, lt))
            mine = here[0] * sizes[1] + here[1]
            for j, step in enumerate(partners):
                copy = pltpu.make_async_remote_copy(
                    src_ref=part_ref,
                    dst_ref=slot_ref.at[mine],
                    send_sem=act_send.at[j],
                    recv_sem=act_recv.at[j],
                    device_id=device(step),
                    device_id_type=MESH,
                )
                copy.start()
                action_copies.append(copy)
            slot_ref[mine] = part_ref[...]

        def fill(wanted):
            for group, source, pair, frm, slot, to, n in fills:
                if group != wanted:
                    continue
                if stage == 0:
                    ref, index = (first_ref, pair) if source is None else (halo_ref, source)
                    halo_ref[slot, :, 0:2, :, to : to + n, :] = ref[index, :, 0:2, :, frm : frm + n, :]
                elif source is None:
                    gen_halo_ref[stage - 1, slot, :, to : to + n, :] = gen_ref[
                        stage - 1, pair, :, frm : frm + n, :
                    ]
                else:
                    gen_halo_ref[stage - 1, slot, :, to : to + n, :] = gen_halo_ref[
                        stage - 1, source, :, frm : frm + n, :
                    ]

        def renew(slot):
            if stage == 0:
                ref = halo_ref.at[slot]
                r, i = ref[0, 0:2], ref[1, 0:2]
                for j in range(3):
                    k, l = (j + 1) % 3, (j + 2) % 3
                    ref[0, 2, j] = (r[0, k] * r[1, l] - i[0, k] * i[1, l]) - (
                        r[0, l] * r[1, k] - i[0, l] * i[1, k]
                    )
                    ref[1, 2, j] = (r[0, l] * i[1, k] + i[0, l] * r[1, k]) - (
                        r[0, k] * i[1, l] + i[0, k] * r[1, l]
                    )
            else:
                new = mul(exponential(gen_halo_ref[stage - 1, slot]), whole(halo_ref, slot))
                halo_ref[slot, 0], halo_ref[slot, 1] = new

        def arrive(group, slots):
            for copy in copies[group]:
                copy.wait_recv()
            fill(group)
            for slot in slots:
                renew(slot)

        def count_action(plaq):
            trace = plaq[0][0, 0] + plaq[0][1, 1] + plaq[0][2, 2]
            term = 1.0 - trace / 3.0
            return term if term.shape[0] == rows else term[:rows] + term[rows:]

        action_terms = []

        def flux_of(one, two):
            plaq = mul_right_adjoint(one, two)
            if stage == 0:
                action_terms.append(count_action(plaq))
            return projected(plaq)

        def centre(d):
            return half(base, *PLACE[d])

        if stage:
            for pair in range(2):
                before = whole(first_ref if stage == 1 else cur_ref, pair)
                moved = mul(exponential(gen_ref[stage - 1, pair]), before)
                cur_ref[pair, 0], cur_ref[pair, 1] = moved
        for d, name in ((X, "x x"), (T, "t t"), (Z, "z z")):
            twice(name, centre(d))
        for d, name in ((X, "x ahead"), (T, "t ahead"), (Y, "y z ahead")):
            keep_half(name, 1, roll(centre(d), -1))

        arrive("y", range(BEHIND[Y], Y_AHEAD + 2))
        for d, name in ((X, "x ahead"), (T, "t ahead"), (Z, "y z ahead")):
            keep_half(name, 0, face(Y, 1, d))
        twice("y behind", face(Y, 0, Y))
        yz = whole(base, 1)
        keep("yx zx", mul(yz, kept("x ahead")))
        keep("yt zt", mul(yz, kept("t ahead")))
        keep("yz zy", mul(yz, kept("y z ahead")))
        one = kept_half("yz zy", 0)
        flux = flux_of(one, kept_half("yz zy", 1))
        flux_ref[1, :, low(0), :] = flux
        flux_ref[1, :, low(1), :] = -flux
        keep_half("lower b", 0, roll(mul_left_adjoint(one, centre(Z)), 1))
        behind = face(Y, 0, Y)
        one = mul(face(Y, 0, Z), roll(behind, -1))
        keep_half("lower b", 1, mul_left_adjoint(one, behind))

        arrive("t", (BEHIND[T], BEHIND[T] + 1, T_AHEAD))
        one = mul(kept("t t"), whole(halo_ref, T_AHEAD))
        keep("ty tz", one)
        flux_t = flux_of(one, kept("yt zt"))
        flux_ref[2] = flux_t
        keep_half("xz tz", 1, kept_half("ty tz", 1))
        behind = face(T, 0, T)
        twice("t behind", behind)
        keep_half("t corner", 1, roll(behind, -1))
        keep_half("behind n", 0, behind)
        keep_half("behind m", 0, face(T, 0, X))

        fill("x")
        for copy in copies["x"]:
            copy.wait_recv()
        for slot in (BEHIND[X], BEHIND[X] + 1, X_AHEAD, BOTH):
            renew(slot)
        one = mul(kept("x x"), whole(halo_ref, X_AHEAD))
        keep("xy xz", one)
        flux_x = flux_of(one, kept("yx zx"))
        flux_ref[3] = flux_x
        keep_half("xz tz", 0, kept_half("xy xz", 1))
        keep_half("t x", 0, half(halo_ref, BOTH, 1))
        keep_half("t x", 1, half(halo_ref, BOTH, 0))
        keep("xt tx", mul(whole(base, 0), kept("t x")))
        flux = flux_of(kept_half("xt tx", 0), kept_half("xt tx", 1))
        flux_ref[0, :, low(0), :] = flux_ref[3, :, low(0), :] + flux_ref[3, :, low(1), :] + flux
        flux_ref[0, :, low(1), :] = flux_ref[2, :, low(0), :] + flux_ref[2, :, low(1), :] - flux
        behind = face(X, 0, X)
        twice("x behind", behind)
        keep_half("x corner", 1, roll(behind, -1))
        keep_half("behind n", 1, behind)
        keep_half("behind m", 1, face(X, 0, T))
        lower_a = roll(mul_left_adjoint(kept("xz tz"), kept("z z")), 1)

        arrive("c", (12, 13))
        keep_half("x corner", 0, half(halo_ref, 13, 0))
        keep_half("t corner", 0, half(halo_ref, 13, 1))
        lower_b = kept("lower b")
        one = mul(whole(halo_ref, BEHIND[X] + 1), kept("x corner"))
        lower_b = add(lower_b, mul_left_adjoint(one, kept("x behind")))
        one = mul(whole(halo_ref, BEHIND[T] + 1), kept("t corner"))
        lower_b = add(lower_b, mul_left_adjoint(one, kept("t behind")))
        one = mul(whole(halo_ref, BEHIND[Y]), whole(halo_ref, 12))
        lower_a = add(lower_a, mul_left_adjoint(one, kept("y behind")))
        keep("lower a", lower_a)

        def finish(pair, lower, upper):
            own = whole(base, pair)
            omega = projected(mul(own, lower)) + upper
            gen = (-flow_eps * FRESH[stage]) * omega
            if stage:
                gen = gen + KEPT[stage] * gen_ref[stage - 1, pair]
            if stage < 2:
                gen_ref[stage, pair] = gen
            else:
                keep("moved %d" % pair, mul(exponential(gen), own))
                for d, (p, pos) in PLACE.items():
                    if p == pair:
                        out_ref[d, 0], out_ref[d, 1] = kept_half("moved %d" % pair, pos)

        finish(1, lower_b, flux_ref[1] - flux_ref[2] - flux_ref[3])
        arrive("xt", (11,))
        one = mul(kept("behind m"), whole(halo_ref, 11))
        lower_a = add(kept("lower a"), mul_left_adjoint(one, kept("behind n")))
        finish(0, lower_a, flux_ref[0])
        if stage == 0:
            action = sum(action_terms)
    assert len(stacks) <= stack_ref.shape[0]
    for copy in started:
        copy.wait_send()
    for copy in action_copies:
        copy.wait()
    total = sum(slot_ref[j] for j in range(sizes[0] * sizes[1]))
    scale = 1.0 / (6.0 * sizes[0] * sizes[1] * block[0] * block[1] * lanes)
    total = jnp.sum(total, axis=1, keepdims=True) * scale
    act_ref[...] = jnp.broadcast_to(total, act_ref.shape)


STACKS = 26
VMEM_LIMIT = 48 * 2**20


def solution(mesh):
    sizes = tuple(mesh.shape[axis] for axis in AXES)

    def local(links):
        block = links.shape[4:7]
        lanes = links.shape[7]
        rows = block[0] * block[1] * block[2]
        plan = plan_of(block)
        partners = [
            (i, j, 0) for i in range(sizes[0]) for j in range(sizes[1]) if i or j
        ]
        count = len(plan[0])
        matrix = (2, 3, 3, rows, lanes)
        both = (2, 3, 3, 2 * rows, lanes)
        f32 = jnp.float32
        vmem = pl.BlockSpec(memory_space=pltpu.VMEM)
        flowed, action = pl.pallas_call(
            functools.partial(kernel, block, sizes, plan, partners),
            out_shape=(
                jax.ShapeDtypeStruct((4,) + matrix, f32),
                jax.ShapeDtypeStruct((block[2], lanes), f32),
            ),
            in_specs=[pl.BlockSpec(memory_space=pltpu.HBM)],
            out_specs=(vmem, vmem),
            scratch_shapes=[
                pltpu.VMEM((2,) + both, f32),
                pltpu.VMEM((2,) + both, f32),
                pltpu.VMEM((SLOTS,) + both, f32),
                pltpu.VMEM((2, 2, 8, 2 * rows, lanes), f32),
                pltpu.VMEM((2, SLOTS, 8, 2 * rows, lanes), f32),
                pltpu.VMEM((STACKS,) + both, f32),
                pltpu.VMEM((4, 8, 2 * rows, lanes), f32),
                pltpu.VMEM((block[2], lanes), f32),
                pltpu.VMEM((sizes[0] * sizes[1], block[2], lanes), f32),
                pltpu.SemaphoreType.DMA((3, count)),
                pltpu.SemaphoreType.DMA((3, count)),
                pltpu.SemaphoreType.DMA((len(partners),)),
                pltpu.SemaphoreType.DMA((len(partners),)),
                pltpu.SemaphoreType.DMA((4,)),
            ],
            compiler_params=pltpu.CompilerParams(
                collective_id=0, has_side_effects=True, vmem_limit_bytes=VMEM_LIMIT
            ),
        )(links.reshape((4,) + matrix))
        return flowed.reshape(links.shape), action[:, 0]

    spec = P(None, None, None, None, "gx", "gy", "ta", None)
    return jax.shard_map(
        local, mesh=mesh, in_specs=(spec,), out_specs=(spec, P("ta")), check_vma=False
    )
```

time: 31.6 us -> 31.1 us (0.984)
  Pallas kernels: 28.1 us -> 27.5 us
    pallas_call x1, Pallas kernels: 28.1 us -> 27.5 us  [local(): pl.pallas_call(functools.partial(kernel, block, sizes, plan, partners), o...]
where the time goes in v1:
time: 31.1 us; the launch traced here: 30.9 us
  Pallas kernels  27.5 us (88%)
  between operations  1.81 us (6%)
  local copies, waits for them, and re-layouts  1.57 us (5%)
    pallas_call x1, Pallas kernels, local(): pl.pallas_call(functools.partial(kernel, block, sizes, plan, partners), o...  27.5 us
    unnamed x3, local copies, waits for them, and re-layouts  1.57 us

profile of v1, /device:TPU:0, one launch (start us, length us, event | category | flops | bytes accessed | tf_op | source)
XLA Modules:
  0.0 30.9 jit_solution(10065677328263141230)
XLA Ops:
  0.6 0.0 copy-start
  0.6 0.9 %copy-done = f32[4,2,3,3,2,2,1,128]{7,6,5,4,3,2,1,0:T(1,128)S(1)} copy-done((f32[4,2,3,3,2,2,1,128]{7,6,5,4,3,2,1,0:T(1,128)S(1)}, f32[4,2,3,3,2,2,1,128]{7,6,5,4,3,2,1,0:T(1,128)}, u32[]{:S(2)}) %copy-start) | copy-done | bytes 147480
  1.5 27.5 %shard_map.30 = (f32[4,2,3,3,4,128]{5,4,3,2,1,0:T(4,128)S(1)}, f32[1,128]{1,0:T(1,128)S(1)}) custom-call(f32[4,2,3,3,4,128]{5,4,3,2,1,0:T(4,128)S(1)} %bitcast.6), custom_call_target="tpu_custom_call" | custom-call | tf_op jit(solution)/shard_map/pallas_call | solution.py:536
  29.1 0.7 %copy.6 = f32[4,2,3,3,2,2,1,128]{7,6,5,4,3,2,1,0:T(1,128)} copy(f32[4,2,3,3,2,2,1,128]{7,6,5,4,3,2,1,0:T(1,128)S(1)} %bitcast.7) | data formatting | bytes 294912
Async XLA Ops:
  0.6 0.9 %copy-start = (f32[4,2,3,3,2,2,1,128]{7,6,5,4,3,2,1,0:T(1,128)S(1)}, f32[4,2,3,3,2,2,1,128]{7,6,5,4,3,2,1,0:T(1,128)}, u32[]{:S(2)}) copy-start(f32[4,2,3,3,2,2,1,128]{7,6,5,4,3,2,1,0:T(1,128)} %param.1) | copy-start | bytes 442372

commit v2 on v1

--- a/solution.py
+++ b/solution.py
@@ -110,6 +110,63 @@
     )
 
 
+def chart(x, rest):
+    length = sum(y * y for y in rest)
+    first = jnp.where(length < 1e-30, 1e-15, rest[0])
+    length = jnp.maximum(length, 1e-30)
+    scale = jnp.where(x < 0.0, 1.0 - x, 1.0) / jnp.where(x < 0.0, length, 1.0 + x)
+    return [scale * y for y in [first] + rest[1:]]
+
+
+def frame(y):
+    q = 2.0 / (1.0 + sum(v * v for v in y))
+    return q, q / (1.0 + y[0] * y[0])
+
+
+def encode(w):
+    r, i = w
+    y = chart(r[0, 0], [i[0, 0], r[0, 1], i[0, 1], r[0, 2], i[0, 2]])
+    f = frame(y)[1]
+    kr = r[1, 0] + y[0] * i[1, 0] + y[1] * r[1, 1] + y[2] * i[1, 1] + y[3] * r[1, 2] + y[4] * i[1, 2]
+    ki = i[1, 0] - y[0] * r[1, 0] + y[1] * i[1, 1] - y[2] * r[1, 1] + y[3] * i[1, 2] - y[4] * r[1, 2]
+    mr, mi = f * (kr + y[0] * ki), f * (ki - y[0] * kr)
+    g = []
+    for k in (1, 2):
+        u, v = y[2 * k - 1], y[2 * k]
+        g += [r[1, k] - (u * mr - v * mi), i[1, k] - (u * mi + v * mr)]
+    return jnp.stack(y + chart(g[0], g[1:]))
+
+
+def decode(code):
+    y, z = [code[k] for k in range(5)], [code[k] for k in range(5, 8)]
+    q, f = frame(y)
+    t = 2.0 / (1.0 + sum(v * v for v in z))
+    g = [t - 1.0] + [t * v for v in z]
+    kr = y[1] * g[0] + y[2] * g[1] + y[3] * g[2] + y[4] * g[3]
+    ki = y[1] * g[1] - y[2] * g[0] + y[3] * g[3] - y[4] * g[2]
+    mr, mi = f * (kr - y[0] * ki), f * (ki + y[0] * kr)
+    r = [[q - 1.0, q * y[1], q * y[3]], [y[0] * mi - mr]]
+    i = [[q * y[0], q * y[2], q * y[4]], [-mi - y[0] * mr]]
+    for k in (1, 2):
+        u, v = y[2 * k - 1], y[2 * k]
+        r[1].append(g[2 * k - 2] - (u * mr - v * mi))
+        i[1].append(g[2 * k - 1] - (u * mi + v * mr))
+    r.append([])
+    i.append([])
+    for j in range(3):
+        k, l = (j + 1) % 3, (j + 2) % 3
+        r[2].append(
+            (r[0][k] * r[1][l] - i[0][k] * i[1][l]) - (r[0][l] * r[1][k] - i[0][l] * i[1][k])
+        )
+        i[2].append(
+            (r[0][l] * i[1][k] + i[0][l] * r[1][k]) - (r[0][k] * i[1][l] + i[0][k] * r[1][l])
+        )
+    return (
+        jnp.stack([jnp.stack(row) for row in r]),
+        jnp.stack([jnp.stack(row) for row in i]),
+    )
+
+
 def runs(pairs):
     out = []
     for to, frm in pairs:
@@ -141,7 +198,8 @@
 PLACE = {X: (0, 0), T: (0, 1), Y: (1, 0), Z: (1, 1)}
 BEHIND = {T: 0, X: 3, Y: 7}
 BOTH, T_AHEAD, X_AHEAD, Y_AHEAD = 5, 2, 6, 9
-CORNER = {(X, T): (11, 0), (T, X): (11, 1), (X, Y): (12, 0), (T, Y): (12, 1), (Y, X): (13, 0), (Y, T): (13, 1)}
+CORNER = {(X, T): (11, 0), (T, X): (11, 1), (X, Y): (12, 0), (Y, X): (12, 1), (T, Y): (13, 0), (Y, T): (13, 1)}
+SEND_ORDER = ("xt", "yt", "xy", "ahead", "behind a", "behind b", "x", "y")
 SLOTS = 14
 
 
@@ -171,7 +229,7 @@
 
     for k in range(3):
         for half, sign in ((0, -1), (1, 1)):
-            group = "xyt"[k]
+            group = "xy"[k] if k < T else "ahead"
             for step, pairs in neighbour_rows(block, unit(k, sign)).items():
                 if any(step):
                     to, frm, n = cover(pairs)
@@ -187,13 +245,16 @@
                         send(group, 0, 1, frm, n, BOTH, to, step)
                         send(group, 1, 1, frm, rows + n, T_AHEAD, to, step)
                     else:
-                        send(group, 0, 2, frm, rows + n, BEHIND[T], to, step)
+                        send("behind a", 0, 1, frm, rows + n, BEHIND[T], to, step)
+                        send("behind b", 1, 1, frm, rows + n, BEHIND[T] + 1, to, step)
                     continue
                 for d in range(4):
                     if half and d == k:
                         continue
                     slot, pos = face_at(k, half, d)
                     pair, at = PLACE[d]
+                    if k == T and not half:
+                        group = "behind b" if pair else "behind a"
                     for to, frm, n in runs(pairs):
                         fills.append((group, None, pair, at * rows + frm, slot, pos * rows + to, n))
     for (m, n), (slot, pos) in CORNER.items():
@@ -201,7 +262,7 @@
         rows_ahead = dict(neighbour_rows(block, ahead).get((0, 0, 0), []))
         rows_behind = dict(neighbour_rows(block, behind).get((0, 0, 0), []))
         offset = tuple(ahead[j] + behind[j] for j in range(3))
-        group = "c" if Y in (m, n) else "xt"
+        group = "xt" if Y not in (m, n) else "yt" if T in (m, n) else "xy"
         pair, at = PLACE[n]
         from_minus, from_plus = [], []
         for step, pairs in neighbour_rows(block, offset).items():
@@ -220,7 +281,7 @@
             source, side = face_at(k, half, n)
             for to, frm, count in runs(sorted(found)):
                 fills.append((group, source, 0, side * rows + frm, slot, pos * rows + to, count))
-    remote.sort(key=lambda item: ("xt", "c", "t", "x", "y").index(item[0]))
+    remote.sort(key=lambda item: SEND_ORDER.index(item[0]))
     return remote, fills
 
 
@@ -267,10 +328,13 @@
     barrier = pltpu.get_barrier_semaphore()
     for step in greeted:
         pl.semaphore_signal(barrier, inc=1, device_id=device(step), device_id_type=MESH)
-    pl.semaphore_wait(barrier, len(greeted))
     for load in loads:
         load.wait()
-
+    for pair in range(2):
+        gen_ref[0, pair] = encode((first_ref[pair, 0], first_ref[pair, 1]))
+    pl.semaphore_wait(barrier, len(greeted))
+
+    last = lax.rem(here[1], 2) == 1
     started, action_copies, stacks = [], [], {}
 
     def low(pos):
@@ -313,15 +377,11 @@
 
     for stage in range(3):
         base = first_ref if stage == 0 else cur_ref
-        copies = {}
+        copies, held = {}, []
         for j, (group, pair, pairs, frm, count, slot, to, step) in enumerate(remote):
             span, into = pl.ds(pair, pairs), pl.ds(slot, pairs)
-            if stage == 0:
-                src = first_ref.at[span, :, pl.ds(0, 2), :, pl.ds(frm, count), :]
-                dst = halo_ref.at[into, :, pl.ds(0, 2), :, pl.ds(to, count), :]
-            else:
-                src = gen_ref.at[stage - 1, span, :, pl.ds(frm, count), :]
-                dst = gen_halo_ref.at[stage - 1, into, :, pl.ds(to, count), :]
+            src = gen_ref.at[stage, span, :, pl.ds(frm, count), :]
+            dst = gen_halo_ref.at[stage, into, :, pl.ds(to, count), :]
             copy = pltpu.make_async_remote_copy(
                 src_ref=src,
                 dst_ref=dst,
@@ -330,9 +390,13 @@
                 device_id=device(tuple(-s for s in step)),
                 device_id_type=MESH,
             )
-            copy.start()
             copies.setdefault(group, []).append(copy)
             started.append(copy)
+            if stage in HELD and group in HELD_GROUPS:
+                pl.when(jnp.logical_not(last))(copy.start)
+                held.append(copy)
+            else:
+                copy.start()
 
         if stage == 1:
             lt = block[2]
@@ -356,38 +420,23 @@
             for group, source, pair, frm, slot, to, n in fills:
                 if group != wanted:
                     continue
-                if stage == 0:
-                    ref, index = (first_ref, pair) if source is None else (halo_ref, source)
-                    halo_ref[slot, :, 0:2, :, to : to + n, :] = ref[index, :, 0:2, :, frm : frm + n, :]
-                elif source is None:
-                    gen_halo_ref[stage - 1, slot, :, to : to + n, :] = gen_ref[
-                        stage - 1, pair, :, frm : frm + n, :
-                    ]
-                else:
-                    gen_halo_ref[stage - 1, slot, :, to : to + n, :] = gen_halo_ref[
-                        stage - 1, source, :, frm : frm + n, :
-                    ]
+                ref = gen_ref.at[stage, pair] if source is None else gen_halo_ref.at[stage, source]
+                gen_halo_ref[stage, slot, :, to : to + n, :] = ref[:, frm : frm + n, :]
 
         def renew(slot):
+            code = gen_halo_ref[stage, slot]
             if stage == 0:
-                ref = halo_ref.at[slot]
-                r, i = ref[0, 0:2], ref[1, 0:2]
-                for j in range(3):
-                    k, l = (j + 1) % 3, (j + 2) % 3
-                    ref[0, 2, j] = (r[0, k] * r[1, l] - i[0, k] * i[1, l]) - (
-                        r[0, l] * r[1, k] - i[0, l] * i[1, k]
-                    )
-                    ref[1, 2, j] = (r[0, l] * i[1, k] + i[0, l] * r[1, k]) - (
-                        r[0, k] * i[1, l] + i[0, k] * r[1, l]
-                    )
+                new = decode(code)
             else:
-                new = mul(exponential(gen_halo_ref[stage - 1, slot]), whole(halo_ref, slot))
-                halo_ref[slot, 0], halo_ref[slot, 1] = new
+                new = mul(exponential(code), whole(halo_ref, slot))
+            halo_ref[slot, 0], halo_ref[slot, 1] = new
 
         def arrive(group, slots):
-            for copy in copies[group]:
-                copy.wait_recv()
-            fill(group)
+            if group != "y":
+                for copy in copies[group]:
+                    copy.wait_recv()
+            if group not in ("x", "xy", "yt", "xt"):
+                fill(group)
             for slot in slots:
                 renew(slot)
 
@@ -410,17 +459,27 @@
         if stage:
             for pair in range(2):
                 before = whole(first_ref if stage == 1 else cur_ref, pair)
-                moved = mul(exponential(gen_ref[stage - 1, pair]), before)
+                moved = mul(exponential(gen_ref[stage, pair]), before)
                 cur_ref[pair, 0], cur_ref[pair, 1] = moved
         for d, name in ((X, "x x"), (T, "t t"), (Z, "z z")):
             twice(name, centre(d))
         for d, name in ((X, "x ahead"), (T, "t ahead"), (Y, "y z ahead")):
             keep_half(name, 1, roll(centre(d), -1))
 
+        for copy in copies["y"]:
+            copy.wait_recv()
+        if held:
+
+            @pl.when(last)
+            def _():
+                for copy in held:
+                    copy.start()
+
         arrive("y", range(BEHIND[Y], Y_AHEAD + 2))
         for d, name in ((X, "x ahead"), (T, "t ahead"), (Z, "y z ahead")):
             keep_half(name, 0, face(Y, 1, d))
-        twice("y behind", face(Y, 0, Y))
+        behind = face(Y, 0, Y)
+        twice("y behind", behind)
         yz = whole(base, 1)
         keep("yx zx", mul(yz, kept("x ahead")))
         keep("yt zt", mul(yz, kept("t ahead")))
@@ -430,76 +489,120 @@
         flux_ref[1, :, low(0), :] = flux
         flux_ref[1, :, low(1), :] = -flux
         keep_half("lower b", 0, roll(mul_left_adjoint(one, centre(Z)), 1))
-        behind = face(Y, 0, Y)
         one = mul(face(Y, 0, Z), roll(behind, -1))
         keep_half("lower b", 1, mul_left_adjoint(one, behind))
 
-        arrive("t", (BEHIND[T], BEHIND[T] + 1, T_AHEAD))
-        one = mul(kept("t t"), whole(halo_ref, T_AHEAD))
-        keep("ty tz", one)
-        flux_t = flux_of(one, kept("yt zt"))
-        flux_ref[2] = flux_t
-        keep_half("xz tz", 1, kept_half("ty tz", 1))
-        behind = face(T, 0, T)
-        twice("t behind", behind)
-        keep_half("t corner", 1, roll(behind, -1))
-        keep_half("behind n", 0, behind)
-        keep_half("behind m", 0, face(T, 0, X))
-
         fill("x")
-        for copy in copies["x"]:
-            copy.wait_recv()
-        for slot in (BEHIND[X], BEHIND[X] + 1, X_AHEAD, BOTH):
-            renew(slot)
-        one = mul(kept("x x"), whole(halo_ref, X_AHEAD))
-        keep("xy xz", one)
-        flux_x = flux_of(one, kept("yx zx"))
-        flux_ref[3] = flux_x
-        keep_half("xz tz", 0, kept_half("xy xz", 1))
-        keep_half("t x", 0, half(halo_ref, BOTH, 1))
-        keep_half("t x", 1, half(halo_ref, BOTH, 0))
-        keep("xt tx", mul(whole(base, 0), kept("t x")))
-        flux = flux_of(kept_half("xt tx", 0), kept_half("xt tx", 1))
-        flux_ref[0, :, low(0), :] = flux_ref[3, :, low(0), :] + flux_ref[3, :, low(1), :] + flux
-        flux_ref[0, :, low(1), :] = flux_ref[2, :, low(0), :] + flux_ref[2, :, low(1), :] - flux
-        behind = face(X, 0, X)
-        twice("x behind", behind)
-        keep_half("x corner", 1, roll(behind, -1))
-        keep_half("behind n", 1, behind)
-        keep_half("behind m", 1, face(X, 0, T))
-        lower_a = roll(mul_left_adjoint(kept("xz tz"), kept("z z")), 1)
-
-        arrive("c", (12, 13))
-        keep_half("x corner", 0, half(halo_ref, 13, 0))
-        keep_half("t corner", 0, half(halo_ref, 13, 1))
-        lower_b = kept("lower b")
-        one = mul(whole(halo_ref, BEHIND[X] + 1), kept("x corner"))
-        lower_b = add(lower_b, mul_left_adjoint(one, kept("x behind")))
-        one = mul(whole(halo_ref, BEHIND[T] + 1), kept("t corner"))
-        lower_b = add(lower_b, mul_left_adjoint(one, kept("t behind")))
-        one = mul(whole(halo_ref, BEHIND[Y]), whole(halo_ref, 12))
-        lower_a = add(lower_a, mul_left_adjoint(one, kept("y behind")))
-        keep("lower a", lower_a)
-
-        def finish(pair, lower, upper):
+
+        def sum_into(name, value):
+            keep(name, add(kept(name) if name in begun else None, value))
+            begun.add(name)
+
+        begun = {"lower b"}
+
+        def x_faces():
+            for slot in (BEHIND[X], BEHIND[X] + 1, X_AHEAD):
+                renew(slot)
+            keep("xy xz", mul(kept("x x"), whole(halo_ref, X_AHEAD)))
+            flux_ref[3] = flux_of(kept("xy xz"), kept("yx zx"))
+            keep_half("xz tz", 0, kept_half("xy xz", 1))
+            behind = face(X, 0, X)
+            twice("x behind", behind)
+            keep_half("x corner", 1, roll(behind, -1))
+            keep_half("behind n", 1, behind)
+            keep_half("behind m", 1, face(X, 0, T))
+
+        def t_ahead():
+            renew(T_AHEAD)
+            keep("ty tz", mul(kept("t t"), whole(halo_ref, T_AHEAD)))
+            flux_ref[2] = flux_of(kept("ty tz"), kept("yt zt"))
+            keep_half("xz tz", 1, kept_half("ty tz", 1))
+
+        def x_and_t_ahead():
+            renew(BOTH)
+            keep_half("t x", 0, half(halo_ref, BOTH, 1))
+            keep_half("t x", 1, half(halo_ref, BOTH, 0))
+            keep("xt tx", mul(whole(base, 0), kept("t x")))
+            flux = flux_of(kept_half("xt tx", 0), kept_half("xt tx", 1))
+            flux_ref[0, :, low(0), :] = flux_ref[3, :, low(0), :] + flux_ref[3, :, low(1), :] + flux
+            flux_ref[0, :, low(1), :] = flux_ref[2, :, low(0), :] + flux_ref[2, :, low(1), :] - flux
+            flux_ref[1] = flux_ref[1] - flux_ref[2] - flux_ref[3]
+            sum_into("lower a", roll(mul_left_adjoint(kept("xz tz"), kept("z z")), 1))
+
+        def xy_corner():
+            fill("xy")
+            renew(12)
+            keep_half("y corner", 0, half(halo_ref, 12, 0))
+            keep_half("x corner", 0, half(halo_ref, 12, 1))
+            one = mul(whole(halo_ref, BEHIND[X] + 1), kept("x corner"))
+            sum_into("lower b", mul_left_adjoint(one, kept("x behind")))
+
+        def t_behind():
+            renew(BEHIND[T])
+            behind = face(T, 0, T)
+            twice("t behind", behind)
+            keep_half("t corner", 1, roll(behind, -1))
+            keep_half("behind n", 0, behind)
+            keep_half("behind m", 0, face(T, 0, X))
+
+        def yt_corner():
+            fill("yt")
+            renew(13)
+            keep_half("y corner", 1, half(halo_ref, 13, 0))
+            keep_half("t corner", 0, half(halo_ref, 13, 1))
+
+        def y_lower():
+            one = mul(whole(halo_ref, BEHIND[Y]), kept("y corner"))
+            sum_into("lower a", mul_left_adjoint(one, kept("y behind")))
+
+        def t_lower():
+            renew(BEHIND[T] + 1)
+            one = mul(whole(halo_ref, BEHIND[T] + 1), kept("t corner"))
+            sum_into("lower b", mul_left_adjoint(one, kept("t behind")))
+
+        def xt_lower():
+            fill("xt")
+            renew(11)
+            one = mul(kept("behind m"), whole(halo_ref, 11))
+            sum_into("lower a", mul_left_adjoint(one, kept("behind n")))
+
+        def finish(pair, name):
             own = whole(base, pair)
-            omega = projected(mul(own, lower)) + upper
+            omega = projected(mul(own, kept(name))) + flux_ref[pair]
             gen = (-flow_eps * FRESH[stage]) * omega
             if stage:
-                gen = gen + KEPT[stage] * gen_ref[stage - 1, pair]
+                gen = gen + KEPT[stage] * gen_ref[stage, pair]
             if stage < 2:
-                gen_ref[stage, pair] = gen
+                gen_ref[stage + 1, pair] = gen
             else:
-                keep("moved %d" % pair, mul(exponential(gen), own))
+                keep("moved", mul(exponential(gen), own))
                 for d, (p, pos) in PLACE.items():
                     if p == pair:
-                        out_ref[d, 0], out_ref[d, 1] = kept_half("moved %d" % pair, pos)
-
-        finish(1, lower_b, flux_ref[1] - flux_ref[2] - flux_ref[3])
-        arrive("xt", (11,))
-        one = mul(kept("behind m"), whole(halo_ref, 11))
-        lower_a = add(kept("lower a"), mul_left_adjoint(one, kept("behind n")))
-        finish(0, lower_a, flux_ref[0])
+                        out_ref[d, 0], out_ref[d, 1] = kept_half("moved", pos)
+
+        tasks = [
+            (x_faces, {"x"}),
+            (t_ahead, {"ahead"}),
+            (x_and_t_ahead, {"x", "ahead"}),
+            (xy_corner, {"x", "xy"}),
+            (t_behind, {"behind a"}),
+            (yt_corner, {"yt", "ahead", "behind a"}),
+            (y_lower, {"x", "xy", "yt", "ahead", "behind a"}),
+            (t_lower, {"behind a", "behind b", "yt", "ahead"}),
+            (lambda: finish(1, "lower b"), {"x", "xy", "ahead", "behind a", "behind b", "yt"}),
+            (xt_lower, {"xt", "x", "ahead", "behind a"}),
+            (lambda: finish(0, "lower a"), {"x", "xy", "ahead", "behind a", "yt", "xt"}),
+        ]
+        here_now = set()
+        for groups in ORDER[stage]:
+            for group in groups:
+                arrive(group, ())
+                here_now.add(group)
+            ready = [task for task, needs in tasks if needs <= here_now]
+            tasks = [(task, needs) for task, needs in tasks if not needs <= here_now]
+            for task in ready:
+                task()
+        assert not tasks
         if stage == 0:
             action = sum(action_terms)
     assert len(stacks) <= stack_ref.shape[0]
@@ -514,6 +617,10 @@
 
 
 STACKS = 26
+HELD = ()
+STEPS = (("ahead",), ("x", "xy"), ("behind a", "yt"), ("behind b",), ("xt",))
+ORDER = (STEPS, STEPS, STEPS)
+HELD_GROUPS = ("ahead", "behind a", "behind b")
 VMEM_LIMIT = 48 * 2**20
 
 
@@ -545,8 +652,8 @@
                 pltpu.VMEM((2,) + both, f32),
                 pltpu.VMEM((2,) + both, f32),
                 pltpu.VMEM((SLOTS,) + both, f32),
-                pltpu.VMEM((2, 2, 8, 2 * rows, lanes), f32),
-                pltpu.VMEM((2, SLOTS, 8, 2 * rows, lanes), f32),
+                pltpu.VMEM((3, 2, 8, 2 * rows, lanes), f32),
+                pltpu.VMEM((3, SLOTS, 8, 2 * rows, lanes), f32),
                 pltpu.VMEM((STACKS,) + both, f32),
                 pltpu.VMEM((4, 8, 2 * rows, lanes), f32),
                 pltpu.VMEM((block[2], lanes), f32),

time: 31.1 us -> 27.8 us (0.89)
  Pallas kernels: 27.5 us -> 24.3 us
    pallas_call x1, Pallas kernels: 27.5 us -> 24.3 us  [local(): pl.pallas_call(functools.partial(kernel, block, sizes, plan, partners), o...]
where the time goes in v2:
time: 27.8 us; the launch traced here: 27.7 us
  Pallas kernels  24.3 us (87%)
  between operations  1.81 us (7%)
  local copies, waits for them, and re-layouts  1.57 us (6%)
    pallas_call x1, Pallas kernels, local(): pl.pallas_call(functools.partial(kernel, block, sizes, plan, partners), o...  24.3 us
    unnamed x3, local copies, waits for them, and re-layouts  1.57 us

profile of v2, /device:TPU:0, one launch (start us, length us, event | category | flops | bytes accessed | tf_op | source)
XLA Modules:
  0.0 27.7 jit_solution(10727675468422031722)
XLA Ops:
  0.6 0.0 copy-start
  0.6 0.9 %copy-done = f32[4,2,3,3,2,2,1,128]{7,6,5,4,3,2,1,0:T(1,128)S(1)} copy-done((f32[4,2,3,3,2,2,1,128]{7,6,5,4,3,2,1,0:T(1,128)S(1)}, f32[4,2,3,3,2,2,1,128]{7,6,5,4,3,2,1,0:T(1,128)}, u32[]{:S(2)}) %copy-start) | copy-done | bytes 147480
  1.5 24.3 %shard_map.30 = (f32[4,2,3,3,4,128]{5,4,3,2,1,0:T(4,128)S(1)}, f32[1,128]{1,0:T(1,128)S(1)}) custom-call(f32[4,2,3,3,4,128]{5,4,3,2,1,0:T(4,128)S(1)} %bitcast.6), custom_call_target="tpu_custom_call" | custom-call | tf_op jit(solution)/shard_map/pallas_call | solution.py:643
  25.8 0.7 %copy.6 = f32[4,2,3,3,2,2,1,128]{7,6,5,4,3,2,1,0:T(1,128)} copy(f32[4,2,3,3,2,2,1,128]{7,6,5,4,3,2,1,0:T(1,128)S(1)} %bitcast.7) | data formatting | bytes 294912
Async XLA Ops:
  0.6 0.9 %copy-start = (f32[4,2,3,3,2,2,1,128]{7,6,5,4,3,2,1,0:T(1,128)S(1)}, f32[4,2,3,3,2,2,1,128]{7,6,5,4,3,2,1,0:T(1,128)}, u32[]{:S(2)}) copy-start(f32[4,2,3,3,2,2,1,128]{7,6,5,4,3,2,1,0:T(1,128)} %param.1) | copy-start | bytes 442372

commit v3 on v2

--- a/solution.py
+++ b/solution.py
@@ -304,20 +304,17 @@
     slot_ref,
     send_sem,
     recv_sem,
-    act_send,
-    act_recv,
+    act_sem,
     load_sem,
 ):
     remote, fills = plan
     rows = block[0] * block[1] * block[2]
     lanes = w_hbm.shape[-1]
-    loads = []
     for d, (pair, pos) in PLACE.items():
         load = pltpu.make_async_copy(
-            w_hbm.at[d], first_ref.at[pair, :, :, :, pl.ds(pos * rows, rows), :], load_sem.at[d]
+            w_hbm.at[d], first_ref.at[pair, :, :, :, pl.ds(pos * rows, rows), :], load_sem.at[0]
         )
         load.start()
-        loads.append(load)
     here = [lax.axis_index(axis) for axis in AXES]
 
     def device(step):
@@ -328,14 +325,22 @@
     barrier = pltpu.get_barrier_semaphore()
     for step in greeted:
         pl.semaphore_signal(barrier, inc=1, device_id=device(step), device_id_type=MESH)
-    for load in loads:
-        load.wait()
+    pltpu.make_async_copy(first_ref, first_ref, load_sem.at[0]).wait()
     for pair in range(2):
         gen_ref[0, pair] = encode((first_ref[pair, 0], first_ref[pair, 1]))
     pl.semaphore_wait(barrier, len(greeted))
 
-    last = lax.rem(here[1], 2) == 1
-    started, action_copies, stacks = [], [], {}
+    units, stacks = {}, {}
+
+    def wait_bytes(count, sem):
+        depth = max(k for k in range(1, 2 * rows + 1) if count % k == 0 and count // k <= SLOTS)
+        span = gen_halo_ref.at[0, pl.ds(0, count // depth), :, pl.ds(0, depth), :]
+        pltpu.make_async_copy(span, span, sem).wait()
+
+    def wait_sent(units):
+        for group, count in units.items():
+            wait_bytes(count, send_sem.at[SEND_ORDER.index(group)])
+
 
     def low(pos):
         return slice(pos * rows, (pos + 1) * rows)
@@ -377,43 +382,38 @@
 
     for stage in range(3):
         base = first_ref if stage == 0 else cur_ref
-        copies, held = {}, []
-        for j, (group, pair, pairs, frm, count, slot, to, step) in enumerate(remote):
+        wait_sent(units)
+        units = {}
+        for group, pair, pairs, frm, count, slot, to, step in remote:
             span, into = pl.ds(pair, pairs), pl.ds(slot, pairs)
             src = gen_ref.at[stage, span, :, pl.ds(frm, count), :]
             dst = gen_halo_ref.at[stage, into, :, pl.ds(to, count), :]
             copy = pltpu.make_async_remote_copy(
                 src_ref=src,
                 dst_ref=dst,
-                send_sem=send_sem.at[stage, j],
-                recv_sem=recv_sem.at[stage, j],
+                send_sem=send_sem.at[SEND_ORDER.index(group)],
+                recv_sem=recv_sem.at[stage % 2, SEND_ORDER.index(group)],
                 device_id=device(tuple(-s for s in step)),
                 device_id_type=MESH,
             )
-            copies.setdefault(group, []).append(copy)
-            started.append(copy)
-            if stage in HELD and group in HELD_GROUPS:
-                pl.when(jnp.logical_not(last))(copy.start)
-                held.append(copy)
-            else:
-                copy.start()
+            units[group] = units.get(group, 0) + pairs * count
+            copy.start()
 
         if stage == 1:
             lt = block[2]
             for t in range(lt):
                 part_ref[t : t + 1, :] = sum(action[r : r + 1] for r in range(t, rows, lt))
             mine = here[0] * sizes[1] + here[1]
-            for j, step in enumerate(partners):
+            for step in partners:
                 copy = pltpu.make_async_remote_copy(
                     src_ref=part_ref,
                     dst_ref=slot_ref.at[mine],
-                    send_sem=act_send.at[j],
-                    recv_sem=act_recv.at[j],
+                    send_sem=act_sem.at[0],
+                    recv_sem=act_sem.at[1],
                     device_id=device(step),
                     device_id_type=MESH,
                 )
                 copy.start()
-                action_copies.append(copy)
             slot_ref[mine] = part_ref[...]
 
         def fill(wanted):
@@ -432,9 +432,8 @@
             halo_ref[slot, 0], halo_ref[slot, 1] = new
 
         def arrive(group, slots):
-            if group != "y":
-                for copy in copies[group]:
-                    copy.wait_recv()
+            if group in units:
+                wait_bytes(units[group], recv_sem.at[stage % 2, SEND_ORDER.index(group)])
             if group not in ("x", "xy", "yt", "xt"):
                 fill(group)
             for slot in slots:
@@ -465,15 +464,6 @@
             twice(name, centre(d))
         for d, name in ((X, "x ahead"), (T, "t ahead"), (Y, "y z ahead")):
             keep_half(name, 1, roll(centre(d), -1))
-
-        for copy in copies["y"]:
-            copy.wait_recv()
-        if held:
-
-            @pl.when(last)
-            def _():
-                for copy in held:
-                    copy.start()
 
         arrive("y", range(BEHIND[Y], Y_AHEAD + 2))
         for d, name in ((X, "x ahead"), (T, "t ahead"), (Z, "y z ahead")):
@@ -606,10 +596,10 @@
         if stage == 0:
             action = sum(action_terms)
     assert len(stacks) <= stack_ref.shape[0]
-    for copy in started:
-        copy.wait_send()
-    for copy in action_copies:
-        copy.wait()
+    wait_sent(units)
+    for k in range(2 if partners else 0):
+        span = slot_ref.at[pl.ds(0, len(partners))]
+        pltpu.make_async_copy(span, span, act_sem.at[k]).wait()
     total = sum(slot_ref[j] for j in range(sizes[0] * sizes[1]))
     scale = 1.0 / (6.0 * sizes[0] * sizes[1] * block[0] * block[1] * lanes)
     total = jnp.sum(total, axis=1, keepdims=True) * scale
@@ -617,11 +607,9 @@
 
 
 STACKS = 26
-HELD = ()
 STEPS = (("ahead",), ("x", "xy"), ("behind a", "yt"), ("behind b",), ("xt",))
 ORDER = (STEPS, STEPS, STEPS)
-HELD_GROUPS = ("ahead", "behind a", "behind b")
-VMEM_LIMIT = 48 * 2**20
+VMEM_LIMIT = 55000 * 1024
 
 
 def solution(mesh):
@@ -635,7 +623,6 @@
         partners = [
             (i, j, 0) for i in range(sizes[0]) for j in range(sizes[1]) if i or j
         ]
-        count = len(plan[0])
         matrix = (2, 3, 3, rows, lanes)
         both = (2, 3, 3, 2 * rows, lanes)
         f32 = jnp.float32
@@ -658,11 +645,10 @@
                 pltpu.VMEM((4, 8, 2 * rows, lanes), f32),
                 pltpu.VMEM((block[2], lanes), f32),
                 pltpu.VMEM((sizes[0] * sizes[1], block[2], lanes), f32),
-                pltpu.SemaphoreType.DMA((3, count)),
-                pltpu.SemaphoreType.DMA((3, count)),
-                pltpu.SemaphoreType.DMA((len(partners),)),
-                pltpu.SemaphoreType.DMA((len(partners),)),
-                pltpu.SemaphoreType.DMA((4,)),
+                pltpu.SemaphoreType.DMA((len(SEND_ORDER),)),
+                pltpu.SemaphoreType.DMA((2, len(SEND_ORDER))),
+                pltpu.SemaphoreType.DMA((2,)),
+                pltpu.SemaphoreType.DMA((1,)),
             ],
             compiler_params=pltpu.CompilerParams(
                 collective_id=0, has_side_effects=True, vmem_limit_bytes=VMEM_LIMIT

time: 27.8 us -> 26.1 us (0.939)
  local copies, waits for them, and re-layouts: 1.57 us -> 0.66 us
  Pallas kernels: 24.3 us -> 23.5 us
    unnamed x3 -> x1, local copies, waits for them, and re-layouts: 1.57 us -> 0.66 us
    pallas_call x1, Pallas kernels: 24.3 us -> 23.5 us  [local(): pl.pallas_call(functools.partial(kernel, block, sizes, plan, partners), o...]
where the time goes in v3:
time: 26.1 us; the launch traced here: 25.9 us
  Pallas kernels  23.5 us (90%)
  between operations  1.8 us (7%)
  local copies, waits for them, and re-layouts  0.66 us (3%)
    pallas_call x1, Pallas kernels, local(): pl.pallas_call(functools.partial(kernel, block, sizes, plan, partners), o...  23.5 us
    unnamed x1, local copies, waits for them, and re-layouts  0.66 us

profile of v3, /device:TPU:0, one launch (start us, length us, event | category | flops | bytes accessed | tf_op | source)
XLA Modules:
  0.0 25.9 jit_solution(6849927750080167259)
XLA Ops:
  0.6 23.5 %shard_map.30 = (f32[4,2,3,3,4,128]{5,4,3,2,1,0:T(4,128)S(1)}, f32[1,128]{1,0:T(1,128)S(1)}) custom-call(f32[4,2,3,3,4,128]{5,4,3,2,1,0:T(4,128)} %bitcast.8), custom_call_target="tpu_custom_call" | custom-call | tf_op jit(solution)/shard_map/pallas_call | solution.py:630
  24.1 0.7 %copy.6 = f32[4,2,3,3,2,2,1,128]{7,6,5,4,3,2,1,0:T(1,128)} copy(f32[4,2,3,3,2,2,1,128]{7,6,5,4,3,2,1,0:T(1,128)S(1)} %bitcast.6) | data formatting | bytes 294912

commit v4 on v3

--- a/solution.py
+++ b/solution.py
@@ -196,22 +196,10 @@
 
 X, Y, T, Z = 0, 1, 2, 3
 PLACE = {X: (0, 0), T: (0, 1), Y: (1, 0), Z: (1, 1)}
-BEHIND = {T: 0, X: 3, Y: 7}
-BOTH, T_AHEAD, X_AHEAD, Y_AHEAD = 5, 2, 6, 9
-CORNER = {(X, T): (11, 0), (T, X): (11, 1), (X, Y): (12, 0), (Y, X): (12, 1), (T, Y): (13, 0), (Y, T): (13, 1)}
+BEHIND = {T: 0, Y: 6}
+T_AHEAD, X_PACK, MIXED, Y_AHEAD, XT = 2, 3, 5, 8, 10
+SLOTS = 11
 SEND_ORDER = ("xt", "yt", "xy", "ahead", "behind a", "behind b", "x", "y")
-SLOTS = 14
-
-
-def face_at(k, half, d):
-    pair, pos = PLACE[d]
-    if not half:
-        return BEHIND[k] + pair, pos
-    if k == Y:
-        return Y_AHEAD + pair, pos
-    if pair:
-        return (X_AHEAD if k == X else T_AHEAD), pos
-    return BOTH, int(k == X)
 
 
 def cover(pairs):
@@ -220,51 +208,54 @@
     return to, frm, max(pairs)[0] - to + 1
 
 
+def local_runs(block, k, sign):
+    return runs(neighbour_rows(block, unit(k, sign)).get((0, 0, 0), []))
+
+
 def plan_of(block):
     rows = block[0] * block[1] * block[2]
-    remote, fills = [], []
+    n = rows // block[0]
+    assert block[0] > 1 and block[1] > 1 and block[2] == 1
+    remote, fills, corners = [], [], {}
 
     def send(group, pair, pairs, frm, count, slot, to, step):
         remote.append((group, pair, pairs, frm, count, slot, to, step))
 
     for k in range(3):
         for half, sign in ((0, -1), (1, 1)):
-            group = "xy"[k] if k < T else "ahead"
             for step, pairs in neighbour_rows(block, unit(k, sign)).items():
-                if any(step):
-                    to, frm, n = cover(pairs)
-                    if k == Y:
-                        send(group, 0, 2, frm, rows + n, Y_AHEAD if half else BEHIND[Y], to, step)
-                    elif k == X and half:
-                        send(group, 0, 2, rows + frm, n, BOTH, rows + to, step)
-                        send(group, 1, 1, frm, n, X_AHEAD, to, step)
-                    elif k == X:
-                        send(group, 0, 2, frm, n, BEHIND[X], to, step)
-                        send(group, 0, 2, rows + frm, n, BEHIND[X], rows + to, step)
-                    elif half:
-                        send(group, 0, 1, frm, n, BOTH, to, step)
-                        send(group, 1, 1, frm, rows + n, T_AHEAD, to, step)
-                    else:
-                        send("behind a", 0, 1, frm, rows + n, BEHIND[T], to, step)
-                        send("behind b", 1, 1, frm, rows + n, BEHIND[T] + 1, to, step)
+                if not any(step):
                     continue
-                for d in range(4):
-                    if half and d == k:
-                        continue
-                    slot, pos = face_at(k, half, d)
-                    pair, at = PLACE[d]
-                    if k == T and not half:
-                        group = "behind b" if pair else "behind a"
-                    for to, frm, n in runs(pairs):
-                        fills.append((group, None, pair, at * rows + frm, slot, pos * rows + to, n))
-    for (m, n), (slot, pos) in CORNER.items():
-        ahead, behind = unit(m, 1), unit(n, -1)
+                to, frm, count = cover(pairs)
+                if k == Y:
+                    slot = Y_AHEAD if half else BEHIND[Y]
+                    send("y", 0, 2, frm, rows + count, slot, to, step)
+                elif k == X and half:
+                    send("x", 0, 2, rows + frm, n, X_PACK, 3 * n, step)
+                    send("x", 1, 1, frm, n, X_PACK + 1, 2 * n, step)
+                elif k == X:
+                    send("x", 0, 2, frm, n, X_PACK, 0, step)
+                    send("x", 0, 2, rows + frm, n, X_PACK, n, step)
+                elif half:
+                    send("ahead", 0, 1, frm, rows, MIXED, 0, step)
+                    send("ahead", 1, 1, frm, 2 * rows, T_AHEAD, 0, step)
+                else:
+                    send("behind a", 0, 1, frm, 2 * rows, BEHIND[T], 0, step)
+                    send("behind b", 1, 1, frm, 2 * rows, BEHIND[T] + 1, 0, step)
+    for half, sign in ((0, -1), (1, 1)):
+        for d, (pair, at) in PLACE.items():
+            for to, frm, count in local_runs(block, Y, sign):
+                slot = (Y_AHEAD if half else BEHIND[Y]) + pair
+                fills.append(("y", None, pair, at * rows + frm, slot, at * rows + to, count))
+    free = {"xy": (X_PACK, 2 * n, 3 * n), "yt": (MIXED, rows, 2 * rows)}
+    for m, n_dir in ((X, T), (T, X), (X, Y), (Y, X), (T, Y), (Y, T)):
+        ahead, behind = unit(m, 1), unit(n_dir, -1)
         rows_ahead = dict(neighbour_rows(block, ahead).get((0, 0, 0), []))
         rows_behind = dict(neighbour_rows(block, behind).get((0, 0, 0), []))
         offset = tuple(ahead[j] + behind[j] for j in range(3))
-        group = "xt" if Y not in (m, n) else "yt" if T in (m, n) else "xy"
-        pair, at = PLACE[n]
-        from_minus, from_plus = [], []
+        group = "xt" if Y not in (m, n_dir) else "yt" if T in (m, n_dir) else "xy"
+        pair, at = PLACE[n_dir]
+        from_minus, from_plus, placed = [], [], []
         for step, pairs in neighbour_rows(block, offset).items():
             outer = []
             for to, frm in pairs:
@@ -274,15 +265,22 @@
                     from_plus.append((to, rows_behind[to]))
                 else:
                     outer.append((to, frm))
-            if outer:
-                to, frm, count = cover(outer)
-                send(group, pair, 1, at * rows + frm, count, slot, pos * rows + to, step)
-        for k, half, found in ((n, 0, from_minus), (m, 1, from_plus)):
-            source, side = face_at(k, half, n)
-            for to, frm, count in runs(sorted(found)):
-                fills.append((group, source, 0, side * rows + frm, slot, pos * rows + to, count))
+            for to, frm, count in runs(outer):
+                if group == "xt":
+                    slot, row = XT, int(m == T) * rows + to
+                else:
+                    slot, row, end = free[group]
+                    free[group] = slot, row + count, end
+                    assert row + count <= end
+                    placed.append((to, slot, row, count))
+                send(group, pair, 1, at * rows + frm, count, slot, row, step)
+        corners[m, n_dir] = placed, runs(sorted(from_minus)), runs(sorted(from_plus))
+    for to, frm, count in corners[X, T][1]:
+        fills.append(("xt", BEHIND[T], 0, rows + frm, XT, to, count))
+    for to, frm, count in corners[T, X][2]:
+        fills.append(("xt", MIXED, 0, frm, XT, rows + to, count))
     remote.sort(key=lambda item: SEND_ORDER.index(item[0]))
-    return remote, fills
+    return remote, fills, corners
 
 
 def kernel(
@@ -307,8 +305,9 @@
     act_sem,
     load_sem,
 ):
-    remote, fills = plan
+    remote, fills, corners = plan
     rows = block[0] * block[1] * block[2]
+    n = rows // block[0]
     lanes = w_hbm.shape[-1]
     for d, (pair, pos) in PLACE.items():
         load = pltpu.make_async_copy(
@@ -377,8 +376,12 @@
         return tuple(pltpu.roll(x, shift % lanes, axis=3) for x in pair)
 
     def face(k, side, d):
-        slot, pos = face_at(k, side, d)
-        return half(halo_ref, slot, pos)
+        pair, pos = PLACE[d]
+        return half(halo_ref, (Y_AHEAD if side else BEHIND[k]) + pair, pos)
+
+    def copy_rows(name, to, ref, index, frm, count):
+        slot = stack(name)
+        stack_ref[slot, :, :, :, to : to + count, :] = ref[index, :, :, :, frm : frm + count, :]
 
     for stage in range(3):
         base = first_ref if stage == 0 else cur_ref
@@ -417,11 +420,11 @@
             slot_ref[mine] = part_ref[...]
 
         def fill(wanted):
-            for group, source, pair, frm, slot, to, n in fills:
+            for group, source, pair, frm, slot, to, count in fills:
                 if group != wanted:
                     continue
                 ref = gen_ref.at[stage, pair] if source is None else gen_halo_ref.at[stage, source]
-                gen_halo_ref[stage, slot, :, to : to + n, :] = ref[:, frm : frm + n, :]
+                gen_halo_ref[stage, slot, :, to : to + count, :] = ref[:, frm : frm + count, :]
 
         def renew(slot):
             code = gen_halo_ref[stage, slot]
@@ -434,7 +437,7 @@
         def arrive(group, slots):
             if group in units:
                 wait_bytes(units[group], recv_sem.at[stage % 2, SEND_ORDER.index(group)])
-            if group not in ("x", "xy", "yt", "xt"):
+            if group != "xt":
                 fill(group)
             for slot in slots:
                 renew(slot)
@@ -464,6 +467,15 @@
             twice(name, centre(d))
         for d, name in ((X, "x ahead"), (T, "t ahead"), (Y, "y z ahead")):
             keep_half(name, 1, roll(centre(d), -1))
+
+        for d, (pair, pos) in PLACE.items():
+            for to, frm, count in local_runs(block, X, -1):
+                copy_rows(("xb a", "xb b")[pair], pos * rows + to, base, pair, pos * rows + frm, count)
+            if d == X:
+                continue
+            for to, frm, count in local_runs(block, X, 1):
+                name, at = ("t x", 0) if d == T else ("xa yz", pos * rows)
+                copy_rows(name, at + to, base, pair, pos * rows + frm, count)
 
         arrive("y", range(BEHIND[Y], Y_AHEAD + 2))
         for d, name in ((X, "x ahead"), (T, "t ahead"), (Z, "y z ahead")):
@@ -482,8 +494,6 @@
         one = mul(face(Y, 0, Z), roll(behind, -1))
         keep_half("lower b", 1, mul_left_adjoint(one, behind))
 
-        fill("x")
-
         def sum_into(name, value):
             keep(name, add(kept(name) if name in begun else None, value))
             begun.add(name)
@@ -491,41 +501,55 @@
         begun = {"lower b"}
 
         def x_faces():
-            for slot in (BEHIND[X], BEHIND[X] + 1, X_AHEAD):
+            for slot in (X_PACK, X_PACK + 1):
                 renew(slot)
-            keep("xy xz", mul(kept("x x"), whole(halo_ref, X_AHEAD)))
+            to = cover(sum((p for q, p in neighbour_rows(block, unit(X, 1)).items() if any(q)), []))[0]
+            copy_rows("xa yz", to, halo_ref, X_PACK + 1, 2 * n, n)
+            copy_rows("xa yz", rows + to, halo_ref, X_PACK + 1, 3 * n, n)
+            copy_rows("t x", to, halo_ref, X_PACK, 3 * n, n)
+            to = cover(sum((p for q, p in neighbour_rows(block, unit(X, -1)).items() if any(q)), []))[0]
+            for pos in range(2):
+                copy_rows("xb a", pos * rows + to, halo_ref, X_PACK, pos * n, n)
+                copy_rows("xb b", pos * rows + to, halo_ref, X_PACK + 1, pos * n, n)
+            keep("xy xz", mul(kept("x x"), kept("xa yz")))
             flux_ref[3] = flux_of(kept("xy xz"), kept("yx zx"))
             keep_half("xz tz", 0, kept_half("xy xz", 1))
-            behind = face(X, 0, X)
+            behind = kept_half("xb a", 0)
             twice("x behind", behind)
             keep_half("x corner", 1, roll(behind, -1))
             keep_half("behind n", 1, behind)
-            keep_half("behind m", 1, face(X, 0, T))
+            keep_half("behind m", 1, kept_half("xb a", 1))
+
+        def corner(name, at, m, n_dir, minus, plus):
+            placed, from_minus, from_plus = corners[m, n_dir]
+            for to, slot, row, count in placed:
+                copy_rows(name, at + to, halo_ref, slot, row, count)
+            for found, source in ((from_minus, minus), (from_plus, plus)):
+                for to, frm, count in found:
+                    copy_rows(name, at + to, source[0], source[1], source[2] + frm, count)
+
+        def xy_corner():
+            corner("y corner", 0, X, Y, (halo_ref, BEHIND[Y] + 1, 0), (stack_ref, stacks["xa yz"], 0))
+            corner("x corner", 0, Y, X, (stack_ref, stacks["xb a"], 0), (halo_ref, Y_AHEAD, 0))
+            one = mul(kept("xb b"), kept("x corner"))
+            sum_into("lower b", mul_left_adjoint(one, kept("x behind")))
 
         def t_ahead():
             renew(T_AHEAD)
+            renew(MIXED)
             keep("ty tz", mul(kept("t t"), whole(halo_ref, T_AHEAD)))
             flux_ref[2] = flux_of(kept("ty tz"), kept("yt zt"))
             keep_half("xz tz", 1, kept_half("ty tz", 1))
+            keep_half("t x", 1, half(halo_ref, MIXED, 0))
+            corner("y corner", rows, T, Y, None, (halo_ref, T_AHEAD, 0))
 
         def x_and_t_ahead():
-            renew(BOTH)
-            keep_half("t x", 0, half(halo_ref, BOTH, 1))
-            keep_half("t x", 1, half(halo_ref, BOTH, 0))
             keep("xt tx", mul(whole(base, 0), kept("t x")))
             flux = flux_of(kept_half("xt tx", 0), kept_half("xt tx", 1))
             flux_ref[0, :, low(0), :] = flux_ref[3, :, low(0), :] + flux_ref[3, :, low(1), :] + flux
             flux_ref[0, :, low(1), :] = flux_ref[2, :, low(0), :] + flux_ref[2, :, low(1), :] - flux
             flux_ref[1] = flux_ref[1] - flux_ref[2] - flux_ref[3]
             sum_into("lower a", roll(mul_left_adjoint(kept("xz tz"), kept("z z")), 1))
-
-        def xy_corner():
-            fill("xy")
-            renew(12)
-            keep_half("y corner", 0, half(halo_ref, 12, 0))
-            keep_half("x corner", 0, half(halo_ref, 12, 1))
-            one = mul(whole(halo_ref, BEHIND[X] + 1), kept("x corner"))
-            sum_into("lower b", mul_left_adjoint(one, kept("x behind")))
 
         def t_behind():
             renew(BEHIND[T])
@@ -534,12 +558,7 @@
             keep_half("t corner", 1, roll(behind, -1))
             keep_half("behind n", 0, behind)
             keep_half("behind m", 0, face(T, 0, X))
-
-        def yt_corner():
-            fill("yt")
-            renew(13)
-            keep_half("y corner", 1, half(halo_ref, 13, 0))
-            keep_half("t corner", 0, half(halo_ref, 13, 1))
+            corner("t corner", 0, Y, T, (halo_ref, BEHIND[T], rows), None)
 
         def y_lower():
             one = mul(whole(halo_ref, BEHIND[Y]), kept("y corner"))
@@ -552,8 +571,8 @@
 
         def xt_lower():
             fill("xt")
-            renew(11)
-            one = mul(kept("behind m"), whole(halo_ref, 11))
+            renew(XT)
+            one = mul(kept("behind m"), whole(halo_ref, XT))
             sum_into("lower a", mul_left_adjoint(one, kept("behind n")))
 
         def finish(pair, name):
@@ -571,16 +590,15 @@
                         out_ref[d, 0], out_ref[d, 1] = kept_half("moved", pos)
 
         tasks = [
-            (x_faces, {"x"}),
-            (t_ahead, {"ahead"}),
-            (x_and_t_ahead, {"x", "ahead"}),
+            (t_ahead, {"ahead", "yt"}),
+            (x_faces, {"x", "xy"}),
+            (x_and_t_ahead, {"x", "xy", "ahead", "yt"}),
             (xy_corner, {"x", "xy"}),
-            (t_behind, {"behind a"}),
-            (yt_corner, {"yt", "ahead", "behind a"}),
-            (y_lower, {"x", "xy", "yt", "ahead", "behind a"}),
+            (y_lower, {"x", "xy", "yt", "ahead"}),
+            (t_behind, {"behind a", "ahead", "yt"}),
             (t_lower, {"behind a", "behind b", "yt", "ahead"}),
             (lambda: finish(1, "lower b"), {"x", "xy", "ahead", "behind a", "behind b", "yt"}),
-            (xt_lower, {"xt", "x", "ahead", "behind a"}),
+            (xt_lower, {"xt", "x", "xy", "ahead", "yt", "behind a"}),
             (lambda: finish(0, "lower a"), {"x", "xy", "ahead", "behind a", "yt", "xt"}),
         ]
         here_now = set()
@@ -606,8 +624,8 @@
     act_ref[...] = jnp.broadcast_to(total, act_ref.shape)
 
 
-STACKS = 26
-STEPS = (("ahead",), ("x", "xy"), ("behind a", "yt"), ("behind b",), ("xt",))
+STACKS = 30
+STEPS = (("ahead", "yt"), ("x", "xy"), ("behind a",), ("behind b",), ("xt",))
 ORDER = (STEPS, STEPS, STEPS)
 VMEM_LIMIT = 55000 * 1024
 

time: 26.1 us -> 25.5 us (0.977)
  Pallas kernels: 23.5 us -> 22.9 us
    pallas_call x1, Pallas kernels: 23.5 us -> 22.9 us  [local(): pl.pallas_call(functools.partial(kernel, block, sizes, plan, partners), o...]
where the time goes in v4:
time: 25.5 us; the launch traced here: 25.4 us
  Pallas kernels  22.9 us (90%)
  between operations  1.8 us (7%)
  local copies, waits for them, and re-layouts  0.66 us (3%)
    pallas_call x1, Pallas kernels, local(): pl.pallas_call(functools.partial(kernel, block, sizes, plan, partners), o...  22.9 us
    unnamed x1, local copies, waits for them, and re-layouts  0.66 us

profile of v4, /device:TPU:0, one launch (start us, length us, event | category | flops | bytes accessed | tf_op | source)
XLA Modules:
  0.0 25.4 jit_solution(16431312238344014263)
XLA Ops:
  0.6 22.9 %shard_map.30 = (f32[4,2,3,3,4,128]{5,4,3,2,1,0:T(4,128)S(1)}, f32[1,128]{1,0:T(1,128)S(1)}) custom-call(f32[4,2,3,3,4,128]{5,4,3,2,1,0:T(4,128)} %bitcast.8), custom_call_target="tpu_custom_call" | custom-call | tf_op jit(solution)/shard_map/pallas_call | solution.py:648
  23.5 0.7 %copy.6 = f32[4,2,3,3,2,2,1,128]{7,6,5,4,3,2,1,0:T(1,128)} copy(f32[4,2,3,3,2,2,1,128]{7,6,5,4,3,2,1,0:T(1,128)S(1)} %bitcast.6) | data formatting | bytes 294912

commit v5 on v4

--- a/solution.py
+++ b/solution.py
@@ -309,21 +309,21 @@
     rows = block[0] * block[1] * block[2]
     n = rows // block[0]
     lanes = w_hbm.shape[-1]
+    here = [lax.axis_index(axis) for axis in AXES]
+
+    def device(step):
+        return tuple(lax.rem(here[k] + step[k] + sizes[k], sizes[k]) for k in range(3))
+
+    steps = [item[-1] for item in remote] + partners
+    greeted = sorted({tuple(s % size for s, size in zip(step, sizes)) for step in steps})
+    barrier = pltpu.get_barrier_semaphore()
+    for step in reversed(greeted):
+        pl.semaphore_signal(barrier, inc=1, device_id=device(step), device_id_type=MESH)
     for d, (pair, pos) in PLACE.items():
         load = pltpu.make_async_copy(
             w_hbm.at[d], first_ref.at[pair, :, :, :, pl.ds(pos * rows, rows), :], load_sem.at[0]
         )
         load.start()
-    here = [lax.axis_index(axis) for axis in AXES]
-
-    def device(step):
-        return tuple(lax.rem(here[k] + step[k] + sizes[k], sizes[k]) for k in range(3))
-
-    steps = sorted({item[-1] for item in remote})
-    greeted = steps + partners
-    barrier = pltpu.get_barrier_semaphore()
-    for step in greeted:
-        pl.semaphore_signal(barrier, inc=1, device_id=device(step), device_id_type=MESH)
     pltpu.make_async_copy(first_ref, first_ref, load_sem.at[0]).wait()
     for pair in range(2):
         gen_ref[0, pair] = encode((first_ref[pair, 0], first_ref[pair, 1]))

time: 25.5 us -> 25.4 us (level)
  no operation moved by 1% of the time
where the time goes in v5:
time: 25.4 us; the launch traced here: 25.3 us
  Pallas kernels  22.8 us (90%)
  between operations  1.8 us (7%)
  local copies, waits for them, and re-layouts  0.66 us (3%)
    pallas_call x1, Pallas kernels, local(): pl.pallas_call(functools.partial(kernel, block, sizes, plan, partners), o...  22.8 us
    unnamed x1, local copies, waits for them, and re-layouts  0.66 us

profile of v5, /device:TPU:0, one launch (start us, length us, event | category | flops | bytes accessed | tf_op | source)
XLA Modules:
  0.0 25.3 jit_solution(2117622713401576533)
XLA Ops:
  0.6 22.8 %shard_map.30 = (f32[4,2,3,3,4,128]{5,4,3,2,1,0:T(4,128)S(1)}, f32[1,128]{1,0:T(1,128)S(1)}) custom-call(f32[4,2,3,3,4,128]{5,4,3,2,1,0:T(4,128)} %bitcast.8), custom_call_target="tpu_custom_call" | custom-call | tf_op jit(solution)/shard_map/pallas_call | solution.py:648
  23.4 0.7 %copy.6 = f32[4,2,3,3,2,2,1,128]{7,6,5,4,3,2,1,0:T(1,128)} copy(f32[4,2,3,3,2,2,1,128]{7,6,5,4,3,2,1,0:T(1,128)S(1)} %bitcast.6) | data formatting | bytes 294912

commit v6 on v5

--- a/solution.py
+++ b/solution.py
@@ -247,7 +247,7 @@
             for to, frm, count in local_runs(block, Y, sign):
                 slot = (Y_AHEAD if half else BEHIND[Y]) + pair
                 fills.append(("y", None, pair, at * rows + frm, slot, at * rows + to, count))
-    free = {"xy": (X_PACK, 2 * n, 3 * n), "yt": (MIXED, rows, 2 * rows)}
+    free = {"xy": (X_PACK, 2 * n, 3 * n), "t": (XT, 0, 2 * rows)}
     for m, n_dir in ((X, T), (T, X), (X, Y), (Y, X), (T, Y), (Y, T)):
         ahead, behind = unit(m, 1), unit(n_dir, -1)
         rows_ahead = dict(neighbour_rows(block, ahead).get((0, 0, 0), []))
@@ -266,19 +266,13 @@
                 else:
                     outer.append((to, frm))
             for to, frm, count in runs(outer):
-                if group == "xt":
-                    slot, row = XT, int(m == T) * rows + to
-                else:
-                    slot, row, end = free[group]
-                    free[group] = slot, row + count, end
-                    assert row + count <= end
-                    placed.append((to, slot, row, count))
+                space = "xy" if group == "xy" else "t"
+                slot, row, end = free[space]
+                free[space] = slot, row + count, end
+                assert row + count <= end
+                placed.append((to, slot, row, count))
                 send(group, pair, 1, at * rows + frm, count, slot, row, step)
         corners[m, n_dir] = placed, runs(sorted(from_minus)), runs(sorted(from_plus))
-    for to, frm, count in corners[X, T][1]:
-        fills.append(("xt", BEHIND[T], 0, rows + frm, XT, to, count))
-    for to, frm, count in corners[T, X][2]:
-        fills.append(("xt", MIXED, 0, frm, XT, rows + to, count))
     remote.sort(key=lambda item: SEND_ORDER.index(item[0]))
     return remote, fills, corners
 
@@ -426,19 +420,20 @@
                 ref = gen_ref.at[stage, pair] if source is None else gen_halo_ref.at[stage, source]
                 gen_halo_ref[stage, slot, :, to : to + count, :] = ref[:, frm : frm + count, :]
 
-        def renew(slot):
-            code = gen_halo_ref[stage, slot]
+        def renew(slot, count=2 * rows):
+            code = gen_halo_ref[stage, slot, :, 0:count, :]
             if stage == 0:
                 new = decode(code)
             else:
-                new = mul(exponential(code), whole(halo_ref, slot))
-            halo_ref[slot, 0], halo_ref[slot, 1] = new
+                old = halo_ref[slot, :, :, :, 0:count, :]
+                new = mul(exponential(code), (old[0], old[1]))
+            halo_ref[slot, 0, :, :, 0:count, :] = new[0]
+            halo_ref[slot, 1, :, :, 0:count, :] = new[1]
 
         def arrive(group, slots):
             if group in units:
                 wait_bytes(units[group], recv_sem.at[stage % 2, SEND_ORDER.index(group)])
-            if group != "xt":
-                fill(group)
+            fill(group)
             for slot in slots:
                 renew(slot)
 
@@ -520,28 +515,32 @@
             keep_half("behind n", 1, behind)
             keep_half("behind m", 1, kept_half("xb a", 1))
 
-        def corner(name, at, m, n_dir, minus, plus):
-            placed, from_minus, from_plus = corners[m, n_dir]
-            for to, slot, row, count in placed:
+        def outer(name, at, m, n_dir):
+            for to, slot, row, count in corners[m, n_dir][0]:
                 copy_rows(name, at + to, halo_ref, slot, row, count)
-            for found, source in ((from_minus, minus), (from_plus, plus)):
+
+        def inner(name, at, m, n_dir, minus, plus):
+            for found, source in zip(corners[m, n_dir][1:], (minus, plus)):
                 for to, frm, count in found:
                     copy_rows(name, at + to, source[0], source[1], source[2] + frm, count)
 
         def xy_corner():
-            corner("y corner", 0, X, Y, (halo_ref, BEHIND[Y] + 1, 0), (stack_ref, stacks["xa yz"], 0))
-            corner("x corner", 0, Y, X, (stack_ref, stacks["xb a"], 0), (halo_ref, Y_AHEAD, 0))
+            outer("y corner", 0, X, Y)
+            outer("x corner", 0, Y, X)
+            inner("y corner", 0, X, Y, (halo_ref, BEHIND[Y] + 1, 0), (stack_ref, stacks["xa yz"], 0))
+            inner("x corner", 0, Y, X, (stack_ref, stacks["xb a"], 0), (halo_ref, Y_AHEAD, 0))
             one = mul(kept("xb b"), kept("x corner"))
             sum_into("lower b", mul_left_adjoint(one, kept("x behind")))
 
         def t_ahead():
             renew(T_AHEAD)
-            renew(MIXED)
+            renew(MIXED, rows)
             keep("ty tz", mul(kept("t t"), whole(halo_ref, T_AHEAD)))
             flux_ref[2] = flux_of(kept("ty tz"), kept("yt zt"))
             keep_half("xz tz", 1, kept_half("ty tz", 1))
             keep_half("t x", 1, half(halo_ref, MIXED, 0))
-            corner("y corner", rows, T, Y, None, (halo_ref, T_AHEAD, 0))
+            inner("y corner", rows, T, Y, None, (halo_ref, T_AHEAD, 0))
+            inner("xt corner", rows, T, X, None, (halo_ref, MIXED, 0))
 
         def x_and_t_ahead():
             keep("xt tx", mul(whole(base, 0), kept("t x")))
@@ -558,7 +557,15 @@
             keep_half("t corner", 1, roll(behind, -1))
             keep_half("behind n", 0, behind)
             keep_half("behind m", 0, face(T, 0, X))
-            corner("t corner", 0, Y, T, (halo_ref, BEHIND[T], rows), None)
+            inner("t corner", 0, Y, T, (halo_ref, BEHIND[T], rows), None)
+            inner("xt corner", 0, X, T, (halo_ref, BEHIND[T], rows), None)
+
+        def t_corners():
+            renew(XT)
+            outer("y corner", rows, T, Y)
+            outer("t corner", 0, Y, T)
+            outer("xt corner", 0, X, T)
+            outer("xt corner", rows, T, X)
 
         def y_lower():
             one = mul(whole(halo_ref, BEHIND[Y]), kept("y corner"))
@@ -570,9 +577,7 @@
             sum_into("lower b", mul_left_adjoint(one, kept("t behind")))
 
         def xt_lower():
-            fill("xt")
-            renew(XT)
-            one = mul(kept("behind m"), whole(halo_ref, XT))
+            one = mul(kept("behind m"), kept("xt corner"))
             sum_into("lower a", mul_left_adjoint(one, kept("behind n")))
 
         def finish(pair, name):
@@ -589,17 +594,19 @@
                     if p == pair:
                         out_ref[d, 0], out_ref[d, 1] = kept_half("moved", pos)
 
+        late = {"x", "xy", "ahead", "behind a", "behind b", "yt", "xt"}
         tasks = [
-            (t_ahead, {"ahead", "yt"}),
+            (t_ahead, {"ahead"}),
             (x_faces, {"x", "xy"}),
-            (x_and_t_ahead, {"x", "xy", "ahead", "yt"}),
+            (x_and_t_ahead, {"x", "xy", "ahead"}),
             (xy_corner, {"x", "xy"}),
-            (y_lower, {"x", "xy", "yt", "ahead"}),
-            (t_behind, {"behind a", "ahead", "yt"}),
-            (t_lower, {"behind a", "behind b", "yt", "ahead"}),
-            (lambda: finish(1, "lower b"), {"x", "xy", "ahead", "behind a", "behind b", "yt"}),
-            (xt_lower, {"xt", "x", "xy", "ahead", "yt", "behind a"}),
-            (lambda: finish(0, "lower a"), {"x", "xy", "ahead", "behind a", "yt", "xt"}),
+            (t_behind, {"behind a", "ahead"}),
+            (t_corners, {"yt", "xt"}),
+            (y_lower, late - {"behind b"}),
+            (xt_lower, late - {"behind b"}),
+            (lambda: finish(0, "lower a"), late - {"behind b"}),
+            (t_lower, late),
+            (lambda: finish(1, "lower b"), late),
         ]
         here_now = set()
         for groups in ORDER[stage]:
@@ -625,7 +632,7 @@
 
 
 STACKS = 30
-STEPS = (("ahead", "yt"), ("x", "xy"), ("behind a",), ("behind b",), ("xt",))
+STEPS = (("ahead",), ("x", "xy"), ("behind a", "yt", "xt"), ("behind b",))
 ORDER = (STEPS, STEPS, STEPS)
 VMEM_LIMIT = 55000 * 1024
 

time: 25.4 us -> 25.2 us (level)
  Pallas kernels: 22.8 us -> 22.5 us
    pallas_call x1, Pallas kernels: 22.8 us -> 22.5 us  [local(): pl.pallas_call(functools.partial(kernel, block, sizes, plan, partners), o...]
where the time goes in v6:
time: 25.2 us; the launch traced here: 25 us
  Pallas kernels  22.5 us (89%)
  between operations  1.8 us (7%)
  local copies, waits for them, and re-layouts  0.66 us (3%)
    pallas_call x1, Pallas kernels, local(): pl.pallas_call(functools.partial(kernel, block, sizes, plan, partners), o...  22.5 us
    unnamed x1, local copies, waits for them, and re-layouts  0.66 us

profile of v6, /device:TPU:0, one launch (start us, length us, event | category | flops | bytes accessed | tf_op | source)
XLA Modules:
  0.0 25.0 jit_solution(5128305929048704227)
XLA Ops:
  0.6 22.5 %shard_map.30 = (f32[4,2,3,3,4,128]{5,4,3,2,1,0:T(4,128)S(1)}, f32[1,128]{1,0:T(1,128)S(1)}) custom-call(f32[4,2,3,3,4,128]{5,4,3,2,1,0:T(4,128)} %bitcast.8), custom_call_target="tpu_custom_call" | custom-call | tf_op jit(solution)/shard_map/pallas_call | solution.py:655
  23.1 0.7 %copy.6 = f32[4,2,3,3,2,2,1,128]{7,6,5,4,3,2,1,0:T(1,128)} copy(f32[4,2,3,3,2,2,1,128]{7,6,5,4,3,2,1,0:T(1,128)S(1)} %bitcast.6) | data formatting | bytes 294912

commit v7 on v6

--- a/solution.py
+++ b/solution.py
@@ -330,9 +330,9 @@
         span = gen_halo_ref.at[0, pl.ds(0, count // depth), :, pl.ds(0, depth), :]
         pltpu.make_async_copy(span, span, sem).wait()
 
-    def wait_sent(units):
+    def wait_sent(units, stage):
         for group, count in units.items():
-            wait_bytes(count, send_sem.at[SEND_ORDER.index(group)])
+            wait_bytes(count, send_sem.at[stage % 2, SEND_ORDER.index(group)])
 
 
     def low(pos):
@@ -379,8 +379,7 @@
 
     for stage in range(3):
         base = first_ref if stage == 0 else cur_ref
-        wait_sent(units)
-        units = {}
+        sent, units = units, {}
         for group, pair, pairs, frm, count, slot, to, step in remote:
             span, into = pl.ds(pair, pairs), pl.ds(slot, pairs)
             src = gen_ref.at[stage, span, :, pl.ds(frm, count), :]
@@ -388,7 +387,7 @@
             copy = pltpu.make_async_remote_copy(
                 src_ref=src,
                 dst_ref=dst,
-                send_sem=send_sem.at[SEND_ORDER.index(group)],
+                send_sem=send_sem.at[stage % 2, SEND_ORDER.index(group)],
                 recv_sem=recv_sem.at[stage % 2, SEND_ORDER.index(group)],
                 device_id=device(tuple(-s for s in step)),
                 device_id_type=MESH,
@@ -472,6 +471,7 @@
                 name, at = ("t x", 0) if d == T else ("xa yz", pos * rows)
                 copy_rows(name, at + to, base, pair, pos * rows + frm, count)
 
+        wait_sent(sent, stage - 1)
         arrive("y", range(BEHIND[Y], Y_AHEAD + 2))
         for d, name in ((X, "x ahead"), (T, "t ahead"), (Z, "y z ahead")):
             keep_half(name, 0, face(Y, 1, d))
@@ -621,7 +621,7 @@
         if stage == 0:
             action = sum(action_terms)
     assert len(stacks) <= stack_ref.shape[0]
-    wait_sent(units)
+    wait_sent(units, 2)
     for k in range(2 if partners else 0):
         span = slot_ref.at[pl.ds(0, len(partners))]
         pltpu.make_async_copy(span, span, act_sem.at[k]).wait()
@@ -670,7 +670,7 @@
                 pltpu.VMEM((4, 8, 2 * rows, lanes), f32),
                 pltpu.VMEM((block[2], lanes), f32),
                 pltpu.VMEM((sizes[0] * sizes[1], block[2], lanes), f32),
-                pltpu.SemaphoreType.DMA((len(SEND_ORDER),)),
+                pltpu.SemaphoreType.DMA((2, len(SEND_ORDER))),
                 pltpu.SemaphoreType.DMA((2, len(SEND_ORDER))),
                 pltpu.SemaphoreType.DMA((2,)),
                 pltpu.SemaphoreType.DMA((1,)),

time: 25.2 us -> 25.2 us (level)
  no operation moved by 1% of the time
where the time goes in v7:
time: 25.2 us; the launch traced here: 25 us
  Pallas kernels  22.5 us (89%)
  between operations  1.8 us (7%)
  local copies, waits for them, and re-layouts  0.66 us (3%)
    pallas_call x1, Pallas kernels, local(): pl.pallas_call(functools.partial(kernel, block, sizes, plan, partners), o...  22.5 us
    unnamed x1, local copies, waits for them, and re-layouts  0.66 us

profile of v7, /device:TPU:0, one launch (start us, length us, event | category | flops | bytes accessed | tf_op | source)
XLA Modules:
  0.0 25.0 jit_solution(8784380757790184665)
XLA Ops:
  0.6 22.5 %shard_map.30 = (f32[4,2,3,3,4,128]{5,4,3,2,1,0:T(4,128)S(1)}, f32[1,128]{1,0:T(1,128)S(1)}) custom-call(f32[4,2,3,3,4,128]{5,4,3,2,1,0:T(4,128)} %bitcast.8), custom_call_target="tpu_custom_call" | custom-call | tf_op jit(solution)/shard_map/pallas_call | solution.py:655
  23.2 0.7 %copy.6 = f32[4,2,3,3,2,2,1,128]{7,6,5,4,3,2,1,0:T(1,128)} copy(f32[4,2,3,3,2,2,1,128]{7,6,5,4,3,2,1,0:T(1,128)S(1)} %bitcast.6) | data formatting | bytes 294912
